TPU v7x, 512 devices: a whole 4x8x8 slice. The times are simulated.
512 devices in a mesh: group: 16 (over z, core), dev: 32 (over x, y).
Axes of the slice: x: 4, y: 8, z: 8, core: 2. Of those that a mesh axis runs over, the one named last changes fastest.
Arguments:
- acts: bfloat16 [196608, 768], P(('group', 'dev')), may hold values from -6 to 6
- grad_out: bfloat16 [196608, 2048], P(('group', 'dev')), may hold values from -0.25 to 0.25
- live_rows: int32 [512], P(('group', 'dev')), may hold values from 96 to 384, as said below
- placement: int32 [512], replicated, may hold values from 0 to 31, as said below
- master: float32 [32, 768, 2048], P('group', 'dev'), may hold values from -0.21875 to 0.21875
- moment1: float32 [32, 768, 2048], P('group', 'dev'), may hold values from -3 to 3
- moment2: float32 [32, 768, 2048], P('group', 'dev'), may hold values from 0.05 to 5
Outputs:
- grad_in: bfloat16 [196608, 768], P(('group', 'dev'))
- new_master: float32 [32, 768, 2048], P('group', 'dev')
- new_moment1: float32 [32, 768, 2048], P('group', 'dev')
- new_moment2: float32 [32, 768, 2048], P('group', 'dev')
Inputs may be any that keep to these rules, and one draw needn't show every extreme that they name: `placement`: every expert is named by some device. In each copy group (devices g * 32 to g * 32 + 31), for every index o of group exactly 2 devices run an expert e with e // 2 = o, and they all run the same one. `live_rows`: some device has all 384 slots live.
All inputs are finite; a program needn't handle non-finite values.
Results may differ from a plain program's by a relative error of at most 0.0085.
Values may be sent and summed in bfloat16 or wider, within the bound.
A program may use at most 64 MiB of HBM per device.

v0:
```python
import jax
import jax.numpy as jnp
from jax import lax
from jax.sharding import PartitionSpec as P

beta_first = 0.9
beta_second = 0.95
learn_rate = 0.02
decay_rate = 0.1
epsilon = 1e-08
correct_first = 1.0 - (0.9**50) ** 2
correct_second = 1.0 - (0.95**50) ** 2


def adam_update(master, moment1, moment2, gradient):
    new_moment1 = beta_first * moment1 + (1.0 - beta_first) * gradient
    new_moment2 = beta_second * moment2 + (1.0 - beta_second) * gradient * gradient
    ascent = new_moment1 / correct_first / (jnp.sqrt(new_moment2 / correct_second) + epsilon)
    new_master = master - learn_rate * (ascent + decay_rate * master)
    return (new_master, new_moment1, new_moment2)


def on_device(acts, grad_out, live_rows, placement, master, moment1, moment2):
    dev_count = lax.axis_size("dev")
    group_count = lax.axis_size("group")
    group_index = lax.axis_index("group")
    roster = lax.dynamic_slice_in_dim(placement, group_index * dev_count, dev_count)
    half_weights = master.astype(jnp.bfloat16)
    per_group = half_weights.shape[0]
    roster_owner = roster // per_group
    everyone = placement.reshape(group_count, dev_count)
    owner_ids = lax.iota(jnp.int32, group_count)
    matches = everyone[:, None, :] // per_group == owner_ids[None, :, None]
    chosen = jnp.max(jnp.where(matches, everyone[:, None, :], -1), axis=2)
    mine = (
        lax.dynamic_index_in_dim(chosen, group_index, 1, keepdims=False) - group_index * per_group
    )
    outgoing = jnp.take(half_weights, mine, axis=0)
    arrived = lax.all_to_all(outgoing, "group", split_axis=0, concat_axis=0, tiled=True)
    selected = jnp.take(arrived, roster_owner, axis=0)
    incoming = lax.all_to_all(selected, "dev", split_axis=0, concat_axis=0, tiled=True)
    full_weight = incoming.reshape(-1, incoming.shape[-1])
    live_mask = (lax.iota(jnp.int32, acts.shape[0]) < live_rows[0])[:, None]
    grad_rows = lax.dot_general(
        grad_out, full_weight, (((1,), (1,)), ((), ())), preferred_element_type=jnp.float32
    )
    grad_in = jnp.where(live_mask, grad_rows, jnp.zeros((), jnp.float32)).astype(jnp.bfloat16)
    masked_acts = jnp.where(live_mask, acts, jnp.zeros((), jnp.bfloat16))
    copy_grad = lax.dot_general(
        masked_acts, grad_out, (((0,), (0,)), ((), ())), preferred_element_type=jnp.float32
    ).astype(jnp.bfloat16)
    returned = lax.all_to_all(
        copy_grad.reshape(selected.shape), "dev", split_axis=0, concat_axis=0, tiled=True
    )
    owner_select = (lax.iota(jnp.int32, group_count)[:, None] == roster_owner[None, :]).astype(
        jnp.bfloat16
    )
    group_slots = jnp.einsum(
        "ov,vpd->opd", owner_select, returned, preferred_element_type=jnp.float32
    ).astype(jnp.bfloat16)
    gathered = lax.all_to_all(group_slots, "group", split_axis=0, concat_axis=0, tiled=True)
    local_ids = group_index * per_group + lax.iota(jnp.int32, per_group)
    fold_select = (local_ids[:, None] == mine[None, :] + group_index * per_group).astype(
        jnp.float32
    )
    gradient = jnp.einsum(
        "jg,gpd->jpd", fold_select, gathered.astype(jnp.float32), precision=lax.Precision.HIGHEST
    )
    new_master, new_moment1, new_moment2 = adam_update(master, moment1, moment2, gradient)
    return (grad_in, new_master, new_moment1, new_moment2)


def solution(mesh):
    in_specs = (
        P(("group", "dev"), None),
        P(("group", "dev"), None),
        P(("group", "dev")),
        P(),
        P("group", "dev", None),
        P("group", "dev", None),
        P("group", "dev", None),
    )
    out_specs = (
        P(("group", "dev"), None),
        P("group", "dev", None),
        P("group", "dev", None),
        P("group", "dev", None),
    )
    return jax.shard_map(
        on_device, mesh=mesh, in_specs=in_specs, out_specs=out_specs, check_vma=False
    )
```

profile of v0, /device:TPU:6, one launch (start us, length us, event | category | flops | bytes accessed | tf_op | source)
XLA Modules:
  0.0 280.9 jit_solution(8533856521886824218)
XLA Ops:
  0.6 0.0 copy-start
  1.4 0.6 copy-done
  2.1 0.0 copy-start.8
  2.1 4.7 %convolution_convert_fusion = bf16[768,2048]{1,0:T(8,128)(2,1)} fusion(bf16[384,2048]{1,0:T(8,128)(2,1)S(1)} %copy-done, bf16[384,768]{1,0:T(8,128)(2,1)} %param.7, pred[384]{0:T(512)(128)(4,1)S(1)} %iota_compare_fusion.2), kind=kOutput, calls=%fused_computation.2 | convolution fusion | flops 1209827328 | bytes 5308800 | tf_op jit(solution)/shard_map/dot_general | solution.py:49
  6.7 0.0 copy-done.8
  6.7 0.0 copy-start.4
  6.7 10.5 %all-to-all-start.2 = ((bf16[32,24,2048]{2,1,0:T(8,128)(2,1)}), bf16[32,24,2048]{2,1,0:T(8,128)(2,1)}, u32[]{:S(2)}, u32[]{:S(2)}) async-start(bf16[32,24,2048]{2,1,0:T(8,128)(2,1)} %bitcast.15), calls=%async_computation.2 | async-start | bytes 6291456 | tf_op jit(solution)/shard_map/all_to_all | solution.py:52
  17.3 0.0 copy-done.4
  17.3 0.1 compare_and_fusion
  17.4 0.0 copy-start.5
  17.4 72.4 %all-to-all-done.2 = bf16[32,24,2048]{2,1,0:T(8,128)(2,1)} async-done(((bf16[32,24,2048]{2,1,0:T(8,128)(2,1)}), bf16[32,24,2048]{2,1,0:T(8,128)(2,1)}, u32[]{:S(2)}, u32[]{:S(2)}) %all-to-all-start.2) | async-done | bytes 3145760 | tf_op jit(solution)/shard_map/all_to_all | solution.py:52
  89.8 5.4 %fusion.2 = bf16[16,24,2048]{2,0,1:T(8,128)(2,1)S(1)} fusion(bf16[32,24,2048]{2,1,0:T(8,128)(2,1)} %all-to-all-done.2, s32[32]{0:T(128)S(1)} %get-tuple-element.34), kind=kOutput, calls=%fused_computation.6 | convolution fusion | flops 51118592 | bytes 4718720 | tf_op jit(solution)/shard_map/ov,vpd->opd/dot_general | solution.py:58
  95.2 0.0 copy-done.5
  95.2 2.0 copy.62
  97.2 10.4 %all-to-all-start.3 = ((bf16[16,24,2048]{2,1,0:T(8,128)(2,1)}), bf16[16,24,2048]{2,1,0:T(8,128)(2,1)S(1)}, u32[]{:S(2)}, u32[]{:S(2)}) async-start(bf16[16,24,2048]{2,1,0:T(8,128)(2,1)} %copy.62), calls=%async_computation.3 | async-start | bytes 3145728 | tf_op jit(solution)/shard_map/all_to_all | solution.py:61
  107.6 0.0 copy-start.1
  107.6 0.1 broadcast_in_dim_reshape.4
  107.7 0.3 select_reduce_fusion
  108.1 0.2 dynamic-slice_reduce_fusion
  108.3 0.7 and_reduce_fusion
  109.0 0.5 iota_add_fusion
  109.5 36.0 %all-to-all-done.3 = bf16[16,24,2048]{2,1,0:T(8,128)(2,1)S(1)} async-done(((bf16[16,24,2048]{2,1,0:T(8,128)(2,1)}), bf16[16,24,2048]{2,1,0:T(8,128)(2,1)S(1)}, u32[]{:S(2)}, u32[]{:S(2)}) %all-to-all-start.3) | async-done | bytes 1572896 | tf_op jit(solution)/shard_map/all_to_all | solution.py:61
  145.5 0.0 copy-start.2
  145.5 0.0 copy-start.3
  145.5 2.5 fusion.5
  148.0 0.0 copy-done.1
  148.0 0.0 copy-done.2
  148.0 0.0 copy-done.3
  148.0 1.4 multiply_subtract_fusion
  149.4 0.0 copy-start.7
  149.4 0.6 gather_fusion
  150.1 0.0 copy-done.7
  150.1 1.4 broadcast_select_fusion.1
  151.5 0.0 copy-start.6
  151.5 4.9 %all-to-all-start = ((bf16[16,24,2048]{2,1,0:T(8,128)(2,1)}), bf16[16,24,2048]{2,1,0:T(8,128)(2,1)S(1)}, u32[]{:S(2)}, u32[]{:S(2)}) async-start(bf16[16,24,2048]{2,1,0:T(8,128)(2,1)} %broadcast_select_fusion.1), calls=%async_computation | async-start | bytes 3145728 | tf_op jit(solution)/shard_map/all_to_all | solution.py:39
  156.4 0.0 copy-done.6
  156.4 37.8 %all-to-all-done = bf16[16,24,2048]{2,1,0:T(8,128)(2,1)S(1)} async-done(((bf16[16,24,2048]{2,1,0:T(8,128)(2,1)}), bf16[16,24,2048]{2,1,0:T(8,128)(2,1)S(1)}, u32[]{:S(2)}, u32[]{:S(2)}) %all-to-all-start) | async-done | bytes 1572896 | tf_op jit(solution)/shard_map/all_to_all | solution.py:39
  194.3 2.4 gather_fusion.1
  196.6 2.2 broadcast_select_fusion
  198.9 0.0 copy-start.9
  198.9 79.1 %all_to_all.20 = bf16[32,24,2048]{2,1,0:T(8,128)(2,1)S(1)} all-to-all(bf16[32,24,2048]{2,1,0:T(8,128)(2,1)S(1)} %broadcast_select_fusion), channel_id=1, replica_groups=mesh['group'=16,'dev'=32] {'dev'}, dimensions={0} | all-to-all | bytes 6291456 | tf_op jit(solution)/shard_map/all_to_all | solution.py:41
  278.0 0.0 copy-done.9
  278.0 1.8 fusion.8
  279.9 1.1 copy.67
  (5 shorter events, 0.0 us)
Async XLA Ops:
  0.6 1.4 copy-start
  2.1 4.7 %copy-start.8 = (pred[384]{0:T(512)(128)(4,1)}, pred[384]{0:T(512)(128)(4,1)S(1)}, u32[]{:S(2)}) copy-start(pred[384]{0:T(512)(128)(4,1)S(1)} %iota_compare_fusion.2) | copy-start | bytes 1156
  6.7 10.5 %copy-start.4 = (s32[512]{0:T(512)S(1)}, s32[512]{0:T(512)}, u32[]{:S(2)}) copy-start(s32[512]{0:T(512)} %param.10) | copy-start | bytes 6148
  6.7 83.1 %all-to-all-start.2 = ((bf16[32,24,2048]{2,1,0:T(8,128)(2,1)}), bf16[32,24,2048]{2,1,0:T(8,128)(2,1)}, u32[]{:S(2)}, u32[]{:S(2)}) async-start(bf16[32,24,2048]{2,1,0:T(8,128)(2,1)} %bitcast.15), calls=%async_computation.2 | async-start | bytes 6291456 | tf_op jit(solution)/shard_map/all_to_all | solution.py:52
  17.4 77.8 %copy-start.5 = (s32[32]{0:T(128)}, s32[32]{0:T(128)S(1)}, u32[]{:S(2)}) copy-start(s32[32]{0:T(128)S(1)} %get-tuple-element.34) | copy-start | bytes 388
  97.2 48.3 %all-to-all-start.3 = ((bf16[16,24,2048]{2,1,0:T(8,128)(2,1)}), bf16[16,24,2048]{2,1,0:T(8,128)(2,1)S(1)}, u32[]{:S(2)}, u32[]{:S(2)}) async-start(bf16[16,24,2048]{2,1,0:T(8,128)(2,1)} %copy.62), calls=%async_computation.3 | async-start | bytes 3145728 | tf_op jit(solution)/shard_map/all_to_all | solution.py:61
  107.6 40.4 %copy-start.1 = (f32[2,24,2048]{2,1,0:T(8,128)S(1)}, f32[2,24,2048]{2,1,0:T(8,128)}, u32[]{:S(2)}) copy-start(f32[2,24,2048]{2,1,0:T(8,128)} %param.11) | copy-start | bytes 1179652
  145.5 2.5 copy-start.2
  145.5 2.5 copy-start.3
  149.4 0.7 copy-start.7
  151.5 4.9 %copy-start.6 = (s32[32]{0:T(128)S(1)}, s32[32]{0:T(128)}, u32[]{:S(2)}) copy-start(s32[32]{0:T(128)} %copy-done.5) | copy-start | bytes 388
  151.5 42.8 %all-to-all-start = ((bf16[16,24,2048]{2,1,0:T(8,128)(2,1)}), bf16[16,24,2048]{2,1,0:T(8,128)(2,1)S(1)}, u32[]{:S(2)}, u32[]{:S(2)}) async-start(bf16[16,24,2048]{2,1,0:T(8,128)(2,1)} %broadcast_select_fusion.1), calls=%async_computation | async-start | bytes 3145728 | tf_op jit(solution)/shard_map/all_to_all | solution.py:39
  198.9 79.1 %copy-start.9 = (pred[384]{0:T(512)(128)(4,1)S(1)}, pred[384]{0:T(512)(128)(4,1)}, u32[]{:S(2)}) copy-start(pred[384]{0:T(512)(128)(4,1)} %copy-done.8) | copy-start | bytes 1156
where the time goes:
time: 285 us; the launch traced here: 281 us
  waiting for transfers between devices  146 us (51%)
  blocking collectives  79.1 us (28%)
  starting transfers between devices  25.9 us (9%)
  matrix products  14.4 us (5%)
  other arithmetic  6.9 us (2%)
  local copies, waits for them, and re-layouts  6.89 us (2%)
    all_to_all x1, blocking collectives, on_device(): lax.all_to_all(selected, 'dev', split_axis=0, concat_axis=0, tiled=True)  79.1 us
    all_to_all x1, waiting for transfers between devices, on_device(): lax.all_to_all(copy_grad.reshape(selected.shape), 'dev', split_axis=0, co...  72.4 us
    all_to_all x1, waiting for transfers between devices, on_device(): lax.all_to_all(outgoing, 'group', split_axis=0, concat_axis=0, tiled=True)  37.8 us
    all_to_all x1, waiting for transfers between devices, on_device(): lax.all_to_all(group_slots, 'group', split_axis=0, concat_axis=0, tiled=T...  36 us
    all_to_all x1, starting transfers between devices, on_device(): lax.all_to_all(copy_grad.reshape(selected.shape), 'dev', split_axis=0, co...  10.5 us
    all_to_all x1, starting transfers between devices, on_device(): lax.all_to_all(group_slots, 'group', split_axis=0, concat_axis=0, tiled=T...  10.4 us
  transfers between devices with their start and end apart: 3, of which 3 were waited for; matrix products, arithmetic and copies ran while one was open for 1% of the time, Pallas kernels for 0%

commit v1 on v0

v1 whole, which is shorter than its diff:
```python
import functools

import jax
import jax.numpy as jnp
from jax import lax
from jax.experimental import pallas as pl
from jax.experimental.pallas import tpu as pltpu
from jax.sharding import PartitionSpec as P

beta_first = 0.9
beta_second = 0.95
learn_rate = 0.02
decay_rate = 0.1
epsilon = 1e-08
correct_first = 1.0 - (0.9**50) ** 2
correct_second = 1.0 - (0.95**50) ** 2

MESH = pl.DeviceIdType.MESH
NX, NY, NZ = 4, 8, 8


def near_offsets():
    half = NY // 2
    near = half // 2
    both = (half - 1) // 2
    own = [(dx, dy) for dx in range(NX) for dy in range(-near, near + 1)]
    par = [(dx, dy) for dx in range(NX) for dy in range(-both, both + 1)]
    return own, par, near, both


def exchange_kernel(
    place_ref,
    tab_ref,
    half_ref,
    copy_ref,
    weight_ref,
    grad_ref,
    w_all,
    w_send_own,
    w_send_par,
    g_own,
    g_par,
    d_send,
    d_recv,
    r_send,
    r_recv,
    p_send,
    p_recv,
    pair_sem,
    ag_send_sem,
    ag_recv_sem,
    core_send_sem,
    core_recv_sem,
    gdev_send_sem,
    gdev_recv_sem,
    wdev_send_sem,
    wdev_recv_sem,
    d_sem,
    rs_send_sem,
    rs_recv_sem,
    local_sem,
):
    g = lax.axis_index("group")
    v = lax.axis_index("dev")
    z, c = g // 2, g % 2
    x, y = v // NY, v % NY
    half = NY // 2
    own, par, near, both = near_offsets()
    n_own, n_par = len(own), len(par)
    vp = x * NY + lax.rem(y + half, NY)
    members = NX * NY

    def at(dx, dy):
        return lax.rem(x + dx + NX, NX) * NY + lax.rem(y + dy + NY, NY)

    def pair_of(vd):
        return (vd // NY) * NY + lax.rem(vd % NY + half, NY)

    def zmod(k):
        return lax.rem(z + k + NZ, NZ)

    pair_dev = (g, vp)
    core_dev = (z * 2 + 1 - c, v)
    z_dev = ((zmod(1) * 2 + c, v), (zmod(-1) * 2 + c, v))

    def remote(src, dst, ssem, rsem, dev):
        return pltpu.make_async_remote_copy(
            src_ref=src, dst_ref=dst, send_sem=ssem, recv_sem=rsem, device_id=dev, device_id_type=MESH
        )

    barrier = pltpu.get_barrier_semaphore()
    peers = [(g, at(dx, dy)) for dx, dy in own if (dx, dy) != (0, 0)] + [pair_dev, core_dev]
    if NZ > 1:
        peers += list(z_dev)
    for dev in peers:
        pl.semaphore_signal(barrier, inc=1, device_id=dev, device_id_type=MESH)

    zero = jnp.zeros(half_ref.shape[1:], jnp.bfloat16)
    g_own[n_own] = zero
    g_par[n_par] = zero
    d_recv[0, NZ] = zero
    d_recv[1, NZ] = zero

    local = [
        pltpu.make_async_copy(half_ref, w_all.at[0, pl.ds(2 * g, 2)], local_sem.at[0]),
        pltpu.make_async_copy(copy_ref.at[v], g_own.at[own.index((0, 0))], local_sem.at[1]),
        pltpu.make_async_copy(copy_ref.at[vp], g_par.at[par.index((0, 0))], local_sem.at[2]),
    ]
    for cp in local:
        cp.start()
    pl.semaphore_wait(barrier, len(peers))

    sends = []

    def go(cp):
        cp.start()
        sends.append(cp)

    block = pl.ds(2 * g, 2)
    pair_copy = remote(half_ref, w_all.at[1, block], pair_sem.at[0], pair_sem.at[1], pair_dev)
    go(pair_copy)
    hops = ((NZ // 2, (NZ - 1) // 2), ((NZ - 1) // 2, NZ // 2))

    def ag(ring, way, step, src=None):
        k = step - 1
        o = zmod(-k if way == 0 else k) * 2 + c
        part = w_all.at[ring, pl.ds(2 * o, 2)]
        return remote(
            part if src is None else src,
            part,
            ag_send_sem.at[ring, way, k],
            ag_recv_sem.at[ring, way, k],
            z_dev[way],
        )

    def ag_arrived(ring, way, step):
        o = zmod(-step if way == 0 else step) * 2 + c
        part = w_all.at[ring, pl.ds(2 * o, 2)]
        remote(
            part, part, ag_send_sem.at[ring, way, step - 1], ag_recv_sem.at[ring, way, step - 1], z_dev[way]
        ).wait_recv()

    def core_copy(ring, k, src=None):
        o = zmod(-k) * 2 + c
        part = w_all.at[ring, pl.ds(2 * o, 2)]
        return remote(
            part if src is None else src,
            part,
            core_send_sem.at[ring, k],
            core_recv_sem.at[ring, k],
            core_dev,
        )

    def core_arrived(ring, k):
        o = zmod(-k) * 2 + 1 - c
        part = w_all.at[ring, pl.ds(2 * o, 2)]
        remote(part, part, core_send_sem.at[ring, k], core_recv_sem.at[ring, k], core_dev).wait_recv()

    def launch(ring, src):
        for way in (0, 1):
            if hops[ring][way] > 0:
                go(ag(ring, way, 1, src))
        go(core_copy(ring, 0, src))

    def forward(ring, step):
        for way in (0, 1):
            if step <= hops[ring][way]:
                ag_arrived(ring, way, step)
                if step < hops[ring][way]:
                    go(ag(ring, way, step + 1))
                go(core_copy(ring, step if way == 0 else NZ - step))

    launch(0, half_ref)

    g_waits = []

    def g_go(src, dst, s, dev):
        cp = remote(src, dst, gdev_send_sem.at[s], gdev_recv_sem.at[s], dev)
        go(cp)
        g_waits.append(cp)

    order = sorted(own, key=lambda d: (-(min(d[0], NX - d[0]) + abs(d[1])), d))
    for dx, dy in order:
        if (dx, dy) == (0, 0):
            continue
        vd = at(dx, dy)
        s = own.index((dx, dy))
        g_go(copy_ref.at[vd], g_own.at[s], s, (g, vd))
        if (dx, dy) in par:
            s = par.index((dx, dy))
            g_go(copy_ref.at[pair_of(vd)], g_par.at[s], n_own + s, (g, vd))

    steps = NZ // 2
    early = min(2, steps)
    for k in range(1, early + 1):
        forward(0, k)
    pair_copy.wait_recv()
    launch(1, None)
    for k in range(early + 1, steps + 1):
        forward(0, k)
        forward(1, k - early)
    for k in range(max(1, steps - early + 1), steps + 1):
        forward(1, k)
    for cp in local:
        cp.wait()
    for ring in (0, 1):
        for k in range(NZ):
            core_arrived(ring, k)

    w_waits = []

    def w_go(src, dst, s, dev):
        cp = remote(src, dst, wdev_send_sem.at[s], wdev_recv_sem.at[s], dev)
        go(cp)
        w_waits.append(cp)

    for dx, dy in order:
        vd = at(dx, dy)
        e = place_ref[g * members + vd]
        if (dx, dy) == (0, 0):
            weight_ref[v] = w_all[0, e]
            weight_ref[vp] = w_all[1, e]
            continue
        s = own.index((dx, dy))
        w_send_own[s] = w_all[0, e]
        w_go(w_send_own.at[s], weight_ref.at[v], s, (g, vd))
        if (dx, dy) in par:
            s = par.index((dx, dy))
            w_send_par[s] = w_all[1, e]
            w_go(w_send_par.at[s], weight_ref.at[vp], n_own + s, (g, vd))

    for cp in g_waits:
        cp.wait_recv()
    recv = (g_own, g_par)
    d_waits = []
    for h in (1, 0):

        def owner_sum(zz, carry, h=h):
            o = 2 * zz + 1 - c
            first = recv[h][tab_ref[2 * h, o]].astype(jnp.float32)
            second = recv[h][tab_ref[2 * h + 1, o]].astype(jnp.float32)
            d_send[h, zz] = (first + second).astype(jnp.bfloat16)
            return carry

        lax.fori_loop(0, NZ, owner_sum, 0)
        cp = remote(d_send.at[h], d_recv.at[h, pl.ds(0, NZ)], d_sem.at[0, h], d_sem.at[1, h], core_dev)
        go(cp)
        d_waits.append(cp)
    for cp in d_waits:
        cp.wait_recv()

    def chip_sum(h, zt, j):
        e = 2 * (2 * zt + c) + j
        first = recv[h][tab_ref[4 + 2 * h, e]].astype(jnp.float32)
        second = recv[h][tab_ref[5 + 2 * h, e]].astype(jnp.float32)
        return first + second + d_recv[h, tab_ref[8, e]].astype(jnp.float32)

    def rs(h, way, step):
        return remote(
            r_send.at[h, way, step - 1],
            r_recv.at[h, way, step - 1],
            rs_send_sem.at[h, way, step - 1],
            rs_recv_sem.at[h, way, step - 1],
            z_dev[1 - way],
        )

    def rs_step(h, step):
        for way in (0, 1):
            length = hops[h][way]
            if step > length:
                continue
            away = length - step + 1
            zt = zmod(-away if way == 0 else away)
            if step > 1:
                rs(h, way, step - 1).wait_recv()
            for j in (0, 1):
                total = chip_sum(h, zt, j)
                if step > 1:
                    total = total + r_recv[h, way, step - 2, j].astype(jnp.float32)
                r_send[h, way, step - 1, j] = total.astype(jnp.bfloat16)
            go(rs(h, way, step))

    def rs_last(h):
        for way in (0, 1):
            if hops[h][way] > 0:
                rs(h, way, hops[h][way]).wait_recv()

    def home_sum(h, j):
        total = chip_sum(h, z, j)
        for way in (0, 1):
            if hops[h][way] > 0:
                total = total + r_recv[h, way, hops[h][way] - 1, j].astype(jnp.float32)
        return total

    for step in range(1, steps + 1):
        rs_step(1, step)
        rs_step(0, step)
    rs_last(1)
    for j in (0, 1):
        p_send[j] = home_sum(1, j).astype(jnp.bfloat16)
    back = remote(p_send, p_recv, pair_sem.at[2], pair_sem.at[3], pair_dev)
    go(back)
    rs_last(0)
    back.wait_recv()
    for j in (0, 1):
        grad_ref[j] = home_sum(0, j) + p_recv[j].astype(jnp.float32)

    for cp in w_waits:
        cp.wait_recv()
    for cp in sends:
        cp.wait_send()


def exchange(placement, table, half_weights, copy_grad):
    rows, width = half_weights.shape[1:]
    own, par, _, _ = near_offsets()
    n_own, n_par = len(own), len(par)
    owners = 2 * NZ
    steps = max(1, NZ // 2)
    dma = pltpu.SemaphoreType.DMA
    vmem = pl.BlockSpec(memory_space=pltpu.VMEM)
    smem = pl.BlockSpec(memory_space=pltpu.SMEM)

    def blocks(*lead):
        return pltpu.VMEM(lead + (rows, width), jnp.bfloat16)

    return pl.pallas_call(
        exchange_kernel,
        name="exchange",
        out_shape=(
            jax.ShapeDtypeStruct((NX * NY, rows, width), jnp.bfloat16),
            jax.ShapeDtypeStruct((2, rows, width), jnp.float32),
        ),
        in_specs=[smem, smem, vmem, vmem],
        out_specs=(vmem, vmem),
        scratch_shapes=[
            blocks(2, 2 * owners),
            blocks(n_own),
            blocks(n_par),
            blocks(n_own + 1),
            blocks(n_par + 1),
            blocks(2, NZ),
            blocks(2, NZ + 1),
            blocks(2, 2, steps, 2),
            blocks(2, 2, steps, 2),
            blocks(2),
            blocks(2),
            dma((4,)),
            dma((2, 2, steps)),
            dma((2, 2, steps)),
            dma((2, NZ)),
            dma((2, NZ)),
            dma((n_own + n_par,)),
            dma((n_own + n_par,)),
            dma((n_own + n_par,)),
            dma((n_own + n_par,)),
            dma((2, 2)),
            dma((2, 2, steps)),
            dma((2, 2, steps)),
            dma((3,)),
        ],
        compiler_params=pltpu.CompilerParams(
            collective_id=0, has_side_effects=True, vmem_limit_bytes=60 * 2**20
        ),
    )(placement, table, half_weights, copy_grad)


def adam_update(master, moment1, moment2, gradient):
    new_moment1 = beta_first * moment1 + (1.0 - beta_first) * gradient
    new_moment2 = beta_second * moment2 + (1.0 - beta_second) * gradient * gradient
    ascent = new_moment1 / correct_first / (jnp.sqrt(new_moment2 / correct_second) + epsilon)
    new_master = master - learn_rate * (ascent + decay_rate * master)
    return (new_master, new_moment1, new_moment2)


def slot_table(placement):
    own, par, near, both = near_offsets()
    g = lax.axis_index("group")
    v = lax.axis_index("dev")
    x, y = v // NY, v % NY
    members = NX * NY
    owners = 2 * NZ
    everyone = placement.reshape(2 * NZ, members)
    roster = lax.dynamic_index_in_dim(everyone, g, 0, keepdims=False)
    other = lax.dynamic_index_in_dim(everyone, g + 1 - 2 * (g % 2), 0, keepdims=False)
    experts = lax.iota(jnp.int32, 2 * owners)
    spots = lax.iota(jnp.int32, members)[None, :]
    owned = roster[None, :] // 2 == experts[:, None] // 2
    first = jnp.min(jnp.where(owned, spots, members), axis=1)
    second = jnp.max(jnp.where(owned, spots, -1), axis=1)
    runs = jnp.any(roster[None, :] == experts[:, None], axis=1)
    other_runs = jnp.any(other[None, :] == experts[:, None], axis=1)

    def slot(source, reach, none):
        dx = (x - source // NY + NX) % NX
        dy = (y - source % NY + NY + NY // 2) % NY - NY // 2
        found = (dy <= reach) & (dy >= -reach)
        return jnp.where(found, dx * (2 * reach + 1) + dy + reach, none)

    per_owner = jnp.stack(
        [slot(first, near, len(own)), slot(second, near, len(own)), slot(first, both, len(par)), slot(second, both, len(par))]
    )
    none = jnp.array([len(own), len(own), len(par), len(par)], jnp.int32)[:, None]
    per_expert = jnp.where(runs[None, :], per_owner, none)
    beside = jnp.where(other_runs, experts // 4, NZ)
    by_owner = jnp.pad(per_owner[:, ::2], ((0, 0), (0, owners)))
    return jnp.concatenate([by_owner, per_expert, beside[None, :]], axis=0)


def on_device(acts, grad_out, live_rows, placement, master, moment1, moment2):
    half_weights = master.astype(jnp.bfloat16)
    live_mask = (lax.iota(jnp.int32, acts.shape[0]) < live_rows[0])[:, None]
    masked_acts = jnp.where(live_mask, acts, jnp.zeros((), jnp.bfloat16))
    copy_grad = lax.dot_general(
        masked_acts, grad_out, (((0,), (0,)), ((), ())), preferred_element_type=jnp.float32
    ).astype(jnp.bfloat16)
    members = NX * NY
    incoming, gradient = exchange(
        placement,
        slot_table(placement),
        half_weights,
        copy_grad.reshape(members, -1, copy_grad.shape[-1]),
    )
    full_weight = incoming.reshape(-1, incoming.shape[-1])
    grad_rows = lax.dot_general(
        grad_out, full_weight, (((1,), (1,)), ((), ())), preferred_element_type=jnp.float32
    )
    grad_in = jnp.where(live_mask, grad_rows, jnp.zeros((), jnp.float32)).astype(jnp.bfloat16)
    new_master, new_moment1, new_moment2 = adam_update(master, moment1, moment2, gradient)
    return (grad_in, new_master, new_moment1, new_moment2)


def solution(mesh):
    in_specs = (
        P(("group", "dev"), None),
        P(("group", "dev"), None),
        P(("group", "dev")),
        P(),
        P("group", "dev", None),
        P("group", "dev", None),
        P("group", "dev", None),
    )
    out_specs = (
        P(("group", "dev"), None),
        P("group", "dev", None),
        P("group", "dev", None),
        P("group", "dev", None),
    )
    return jax.shard_map(
        on_device, mesh=mesh, in_specs=in_specs, out_specs=out_specs, check_vma=False
    )
```

time: 285 us -> 139 us (0.49)
  the two profiles are of different devices: /device:TPU:6 before, /device:TPU:17 now
where the time goes in v1:
time: 139 us
  Pallas kernels  121 us (87%)
  matrix products  8.44 us (6%)
  other arithmetic  5.7 us (4%)
  local copies, waits for them, and re-layouts  1.96 us (1%)
  between operations  1.51 us (1%)
    pallas_call x1, Pallas kernels, exchange(): pl.pallas_call(exchange_kernel, name='exchange', out_shape=(jax.ShapeDtyp...  121 us
    dot_general x1, matrix products, on_device(): lax.dot_general(masked_acts, grad_out, (((0,), (0,)), ((), ())), preferre...  4.65 us
    dot_general x1, matrix products, on_device(): lax.dot_general(grad_out, full_weight, (((1,), (1,)), ((), ())), preferre...  3.79 us

profile of v1, /device:TPU:17, one launch (start us, length us, event | category | flops | bytes accessed | tf_op | source)
XLA Modules:
  0.0 138.6 jit_solution(18161782666044915316)
XLA Ops:
  0.6 0.0 copy-start
  1.5 0.8 reshape.491
  2.2 0.1 fusion.8
  2.4 0.1 fusion.9
  2.5 0.2 fusion.6
  2.7 0.7 broadcast_select_fusion
  3.4 0.1 slice.3
  3.5 0.6 fusion.10.tab_ref
  4.2 1.7 %convert_element_type.12.half_ref = bf16[2,24,2048]{2,1,0:T(8,128)(2,1)} convert(f32[2,24,2048]{2,1,0:T(8,128)} %param.12) | non-fusion elementwise | flops 98304 | bytes 589824 | tf_op jit(solution)/shard_map/convert_element_type | solution.py:411
  5.9 0.0 copy-done
  5.9 4.7 %convolution_convert_fusion = bf16[768,2048]{1,0:T(8,128)(2,1)} fusion(bf16[384,2048]{1,0:T(8,128)(2,1)S(1)} %copy-done, bf16[384,768]{1,0:T(8,128)(2,1)} %param.8, pred[384]{0:T(512)(128)(4,1)S(1)} %iota_compare_fusion.2), kind=kOutput, calls=%fused_computation | convolution fusion | flops 1209827328 | bytes 5308800 | tf_op jit(solution)/shard_map/dot_general | solution.py:414
  10.5 121.0 %exchange.1 = (bf16[32,24,2048]{2,1,0:T(8,128)(2,1)}, f32[2,24,2048]{2,1,0:T(8,128)}) custom-call(s32[512]{0:T(512)} %place_ref.1, s32[9,32]{1,0:T(8,128)} %fusion.10.tab_ref, bf16[2,24,2048]{2,1,0:T(8,128)(2,1)} %convert_element_type.12.half_ref, bf16[32,24,2048]{2,1,0:T(8,128)(2,1)} %bitcast.67), custom_call_target="tpu_custom_call" | custom-call | tf_op jit(solution)/shard_map/exchange/pallas_call | solution.py:327
  131.5 0.0 copy-start.1
  131.5 0.0 copy-start.2
  131.5 0.0 copy-start.3
  131.5 3.8 %fusion.1 = bf16[384,768]{0,1:T(8,128)(2,1)S(1)} fusion(bf16[768,2048]{1,0:T(8,128)(2,1)} %bitcast.68, bf16[384,2048]{1,0:T(8,128)(2,1)S(1)} %copy-done, pred[384]{0:T(512)(128)(4,1)S(1)} %iota_compare_fusion.2), kind=kOutput, calls=%fused_computation.3 | convolution fusion | flops 1208549376 | bytes 5308800 | tf_op jit(solution)/shard_map/dot_general | solution.py:425
  135.3 1.1 copy.13
  136.4 0.0 copy-done.1
  136.4 0.0 copy-done.2
  136.4 0.0 copy-done.3
  136.4 2.2 %multiply_subtract_fusion = (f32[2,24,2048]{2,1,0:T(8,128)}, f32[2,24,2048]{2,1,0:T(8,128)}, f32[2,24,2048]{2,1,0:T(8,128)}) fusion(f32[2,24,2048]{2,1,0:T(8,128)S(1)} %copy-done.1, f32[2,24,2048]{2,1,0:T(8,128)} %get-tuple-element.7, f32[2,24,2048]{2,1,0:T(8,128)S(1)} %copy-done.2, f32[2,24,2048]{2,1,0:T(8,128)S(1)} %copy-done.3), kind=kLoop, calls=%fused_computation.8 | loop fusion | flops 1474560 | bytes 2752512 | tf_op jit(solution)/shard_map/sub | solution.py:372
  (5 shorter events, 0.1 us)
Async XLA Ops:
  0.6 5.2 %copy-start = (bf16[384,2048]{1,0:T(8,128)(2,1)S(1)}, bf16[384,2048]{1,0:T(8,128)(2,1)}, u32[]{:S(2)}) copy-start(bf16[384,2048]{1,0:T(8,128)(2,1)} %param.9) | copy-start | bytes 4718596
  131.5 4.9 %copy-start.1 = (f32[2,24,2048]{2,1,0:T(8,128)S(1)}, f32[2,24,2048]{2,1,0:T(8,128)}, u32[]{:S(2)}) copy-start(f32[2,24,2048]{2,1,0:T(8,128)} %param.12) | copy-start | bytes 1179652
  131.5 4.9 %copy-start.2 = (f32[2,24,2048]{2,1,0:T(8,128)S(1)}, f32[2,24,2048]{2,1,0:T(8,128)}, u32[]{:S(2)}) copy-start(f32[2,24,2048]{2,1,0:T(8,128)} %param.13) | copy-start | bytes 1179652
  131.5 4.9 %copy-start.3 = (f32[2,24,2048]{2,1,0:T(8,128)S(1)}, f32[2,24,2048]{2,1,0:T(8,128)}, u32[]{:S(2)}) copy-start(f32[2,24,2048]{2,1,0:T(8,128)} %param.14) | copy-start | bytes 1179652

commit v2 on v1

v2 whole, which is shorter than its diff:
```python
import functools

import jax
import jax.numpy as jnp
from jax import lax
from jax.experimental import pallas as pl
from jax.experimental.pallas import tpu as pltpu
from jax.sharding import PartitionSpec as P

beta_first = 0.9
beta_second = 0.95
learn_rate = 0.02
decay_rate = 0.1
epsilon = 1e-08
correct_first = 1.0 - (0.9**50) ** 2
correct_second = 1.0 - (0.95**50) ** 2

MESH = pl.DeviceIdType.MESH
NX, NY, NZ = 4, 8, 8


def near_offsets():
    half = NY // 2
    near = half // 2
    both = (half - 1) // 2
    own = [(dx, dy) for dx in range(NX) for dy in range(-near, near + 1)]
    par = [(dx, dy) for dx in range(NX) for dy in range(-both, both + 1)]
    return own, par, near, both


def step_kernel(
    place_ref,
    tab_ref,
    live_ref,
    acts_ref,
    out_ref,
    master_ref,
    rows_ref,
    grad_ref,
    half_w,
    copy_g,
    weight,
    in_parts,
    w_own,
    w_par,
    w_send_own,
    w_send_par,
    g_own,
    g_par,
    d_send,
    d_own,
    d_par,
    r_send,
    r_recv,
    p_send,
    p_recv,
    pair_sem,
    ag_send_sem,
    ag_recv_sem,
    core_send_sem,
    core_recv_sem,
    gdev_send_sem,
    gdev_recv_sem,
    wdev_send_sem,
    wdev_recv_sem,
    d_sem,
    rs_send_sem,
    rs_recv_sem,
    local_sem,
):
    g = lax.axis_index("group")
    v = lax.axis_index("dev")
    z, c = g // 2, g % 2
    x, y = v // NY, v % NY
    half = NY // 2
    own, par, near, both = near_offsets()
    n_own, n_par = len(own), len(par)
    vp = x * NY + lax.rem(y + half, NY)
    members = NX * NY
    rows, width = half_w.shape[1:]
    w_all, d_recv = (w_own, w_par), (d_own, d_par)

    def at(dx, dy):
        return lax.rem(x + dx + NX, NX) * NY + lax.rem(y + dy + NY, NY)

    def pair_of(vd):
        return (vd // NY) * NY + lax.rem(vd % NY + half, NY)

    def zmod(k):
        return lax.rem(z + k + NZ, NZ)

    pair_dev = (g, vp)
    core_dev = (z * 2 + 1 - c, v)
    z_dev = ((zmod(1) * 2 + c, v), (zmod(-1) * 2 + c, v))

    def remote(src, dst, ssem, rsem, dev):
        return pltpu.make_async_remote_copy(
            src_ref=src, dst_ref=dst, send_sem=ssem, recv_sem=rsem, device_id=dev, device_id_type=MESH
        )

    barrier = pltpu.get_barrier_semaphore()
    peers = [(g, at(dx, dy)) for dx, dy in own if (dx, dy) != (0, 0)] + [pair_dev, core_dev]
    if NZ > 1:
        peers += list(z_dev)
    for dev in peers:
        pl.semaphore_signal(barrier, inc=1, device_id=dev, device_id_type=MESH)

    half_w[...] = master_ref[...].astype(jnp.bfloat16)
    zero = jnp.zeros((rows, width), jnp.bfloat16)
    g_own[n_own] = zero
    g_par[n_par] = zero
    d_own[NZ] = zero
    d_par[NZ] = zero
    pl.semaphore_wait(barrier, len(peers))

    sends = []

    def go(cp):
        cp.start()
        sends.append(cp)

    block = pl.ds(2 * g, 2)
    pair_copy = remote(half_w, w_all[1].at[block], pair_sem.at[0], pair_sem.at[1], pair_dev)
    go(pair_copy)
    hops = ((NZ // 2, (NZ - 1) // 2), ((NZ - 1) // 2, NZ // 2))

    def ag(ring, way, step, src=None):
        k = step - 1
        o = zmod(-k if way == 0 else k) * 2 + c
        part = w_all[ring].at[pl.ds(2 * o, 2)]
        return remote(
            part if src is None else src,
            part,
            ag_send_sem.at[ring, way, k],
            ag_recv_sem.at[ring, way, k],
            z_dev[way],
        )

    def ag_arrived(ring, way, step):
        o = zmod(-step if way == 0 else step) * 2 + c
        part = w_all[ring].at[pl.ds(2 * o, 2)]
        remote(
            part, part, ag_send_sem.at[ring, way, step - 1], ag_recv_sem.at[ring, way, step - 1], z_dev[way]
        ).wait_recv()

    def core_copy(ring, k, src=None):
        o = zmod(-k) * 2 + c
        part = w_all[ring].at[pl.ds(2 * o, 2)]
        return remote(
            part if src is None else src,
            part,
            core_send_sem.at[ring, k],
            core_recv_sem.at[ring, k],
            core_dev,
        )

    def core_arrived(ring):
        for k in range(NZ):
            o = zmod(-k) * 2 + 1 - c
            part = w_all[ring].at[pl.ds(2 * o, 2)]
            remote(part, part, core_send_sem.at[ring, k], core_recv_sem.at[ring, k], core_dev).wait_recv()

    def launch(ring, src):
        for way in (0, 1):
            if hops[ring][way] > 0:
                go(ag(ring, way, 1, src))
        go(core_copy(ring, 0, src))

    def forward(ring, step):
        for way in (0, 1):
            if 1 <= step <= hops[ring][way]:
                ag_arrived(ring, way, step)
                if step < hops[ring][way]:
                    go(ag(ring, way, step + 1))
                go(core_copy(ring, step if way == 0 else NZ - step))

    launch(0, half_w)
    local_w = pltpu.make_async_copy(half_w, w_all[0].at[block], local_sem.at[0])
    local_w.start()

    live = lax.broadcasted_iota(jnp.int32, acts_ref.shape, 0) < live_ref[0]
    masked = jnp.where(live, acts_ref[...], jnp.zeros((), jnp.bfloat16))
    strip = min(512, width)

    def copy_strip(i, carry):
        cols = pl.ds(pl.multiple_of(i * strip, strip), strip)
        product = lax.dot_general(
            masked, out_ref[:, cols], (((0,), (0,)), ((), ())), preferred_element_type=jnp.float32
        )
        copy_g[:, :, cols] = product.astype(jnp.bfloat16).reshape(members, rows, strip)
        return carry

    lax.fori_loop(0, width // strip, copy_strip, 0)

    local_g = [
        pltpu.make_async_copy(copy_g.at[v], g_own.at[own.index((0, 0))], local_sem.at[1]),
        pltpu.make_async_copy(copy_g.at[vp], g_par.at[par.index((0, 0))], local_sem.at[2]),
    ]
    for cp in local_g:
        cp.start()
    g_waits = ([], [])

    def g_go(h, src, dst, s, dev):
        cp = remote(src, dst, gdev_send_sem.at[s], gdev_recv_sem.at[s], dev)
        go(cp)
        g_waits[h].append(cp)

    order = sorted(own, key=lambda d: (-(min(d[0], NX - d[0]) + abs(d[1])), d))
    order = [d for d in order if d != (0, 0)]
    for dx, dy in order:
        if (dx, dy) in par:
            vd = at(dx, dy)
            s = par.index((dx, dy))
            g_go(1, copy_g.at[pair_of(vd)], g_par.at[s], n_own + s, (g, vd))
    for dx, dy in order:
        vd = at(dx, dy)
        s = own.index((dx, dy))
        g_go(0, copy_g.at[vd], g_own.at[s], s, (g, vd))

    w_waits = {}

    def w_go(src, dst, s, dev, dx):
        cp = remote(src, dst, wdev_send_sem.at[s], wdev_recv_sem.at[s], dev)
        go(cp)
        w_waits.setdefault(dx, []).append(cp)

    def deal_own():
        for dx, dy in order:
            vd = at(dx, dy)
            s = own.index((dx, dy))
            w_send_own[s] = w_all[0][place_ref[g * members + vd]]
            w_go(w_send_own.at[s], weight.at[v], s, (g, vd), dx)
        weight[v] = w_all[0][place_ref[g * members + v]]

    def deal_par():
        for dx, dy in order:
            if (dx, dy) in par:
                vd = at(dx, dy)
                s = par.index((dx, dy))
                w_send_par[s] = w_all[1][place_ref[g * members + vd]]
                w_go(w_send_par.at[s], weight.at[vp], n_own + s, (g, vd), dx)
        weight[vp] = w_all[1][place_ref[g * members + v]]

    recv = (g_own, g_par)

    def core_swap(h):
        return remote(d_send.at[h], d_recv[h].at[pl.ds(0, NZ)], d_sem.at[0, h], d_sem.at[1, h], core_dev)

    def give_core(h):
        local_g[h].wait()
        for cp in g_waits[h]:
            cp.wait_recv()

        def owner_sum(zz, carry):
            e = 2 * (2 * zz + 1 - c)
            first = recv[h][tab_ref[4 * h, e]].astype(jnp.float32)
            second = recv[h][tab_ref[4 * h + 1, e]].astype(jnp.float32)
            d_send[h, zz] = (first + second).astype(jnp.bfloat16)
            return carry

        lax.fori_loop(0, NZ, owner_sum, 0)
        go(core_swap(h))

    def chip_sum(h, zt, j):
        e = 2 * (2 * zt + c) + j
        first = recv[h][tab_ref[4 * h + 2, e]].astype(jnp.float32)
        second = recv[h][tab_ref[4 * h + 3, e]].astype(jnp.float32)
        return first + second + d_recv[h][tab_ref[8, e]].astype(jnp.float32)

    def rs(h, way, step):
        return remote(
            r_send.at[h, way, step - 1],
            r_recv.at[h, way, step - 1],
            rs_send_sem.at[h, way, step - 1],
            rs_recv_sem.at[h, way, step - 1],
            z_dev[1 - way],
        )

    def rs_step(h, step):
        for way in (0, 1):
            length = hops[h][way]
            if step > length:
                continue
            away = length - step + 1
            zt = zmod(-away if way == 0 else away)
            if step > 1:
                rs(h, way, step - 1).wait_recv()
            for j in (0, 1):
                total = chip_sum(h, zt, j)
                if step > 1:
                    total = total + r_recv[h, way, step - 2, j].astype(jnp.float32)
                r_send[h, way, step - 1, j] = total.astype(jnp.bfloat16)
            go(rs(h, way, step))

    def rs_last(h):
        for way in (0, 1):
            if hops[h][way] > 0:
                rs(h, way, hops[h][way]).wait_recv()

    def home_sum(h, j):
        total = chip_sum(h, z, j)
        for way in (0, 1):
            if hops[h][way] > 0:
                total = total + r_recv[h, way, hops[h][way] - 1, j].astype(jnp.float32)
        return total

    steps = NZ // 2
    forward(0, 1)
    forward(0, 2)
    pair_copy.wait_recv()
    launch(1, None)
    forward(0, 3)
    forward(1, 1)
    give_core(1)
    for k in range(4, steps + 1):
        forward(0, k)
    forward(1, 2)
    core_swap(1).wait_recv()
    rs_step(1, 1)
    local_w.wait()
    core_arrived(0)
    deal_own()
    forward(1, 3)
    rs_step(1, 2)
    for k in range(4, steps + 1):
        forward(1, k)
    core_arrived(1)
    deal_par()
    rs_step(1, 3)
    give_core(0)
    for step in range(4, steps + 1):
        rs_step(1, step)
    core_swap(0).wait_recv()
    rs_step(0, 1)
    rs_last(1)
    for j in (0, 1):
        p_send[j] = home_sum(1, j).astype(jnp.bfloat16)
    back = remote(p_send, p_recv, pair_sem.at[2], pair_sem.at[3], pair_dev)
    go(back)
    for step in range(2, steps + 1):
        rs_step(0, step)
    rs_last(0)
    back.wait_recv()
    for j in (0, 1):
        grad_ref[j] = home_sum(0, j) + p_recv[j].astype(jnp.float32)

    for dx in sorted(range(NX), key=lambda d: (min(d, NX - d), d)):
        for cp in w_waits.get(dx, []):
            cp.wait_recv()
        xs = lax.rem(x - dx + NX, NX)
        part = weight[pl.ds(xs * NY, NY)].reshape(NY * rows, width)
        in_parts[xs] = lax.dot_general(
            out_ref[...], part, (((1,), (1,)), ((), ())), preferred_element_type=jnp.float32
        ).astype(jnp.bfloat16)
    for xs in range(NX):
        rows_ref[:, xs * NY * rows : (xs + 1) * NY * rows] = in_parts[xs]
    for cp in sends:
        cp.wait_send()


def step(placement, table, live_rows, acts, grad_out, master):
    rows, width = master.shape[1:]
    own, par, _, _ = near_offsets()
    n_own, n_par = len(own), len(par)
    owners = 2 * NZ
    steps = max(1, NZ // 2)
    dma = pltpu.SemaphoreType.DMA
    vmem = pl.BlockSpec(memory_space=pltpu.VMEM)
    smem = pl.BlockSpec(memory_space=pltpu.SMEM)

    def blocks(*lead):
        return pltpu.VMEM(lead + (rows, width), jnp.bfloat16)

    return pl.pallas_call(
        step_kernel,
        name="step",
        out_shape=(
            jax.ShapeDtypeStruct(acts.shape, jnp.bfloat16),
            jax.ShapeDtypeStruct(master.shape, jnp.float32),
        ),
        in_specs=[smem, smem, smem, vmem, vmem, vmem],
        out_specs=(vmem, vmem),
        scratch_shapes=[
            blocks(2),
            blocks(NX * NY),
            blocks(NX * NY),
            pltpu.VMEM((NX, acts.shape[0], NY * rows), jnp.bfloat16),
            blocks(2 * owners),
            blocks(2 * owners),
            blocks(n_own),
            blocks(n_par),
            blocks(n_own + 1),
            blocks(n_par + 1),
            blocks(2, NZ),
            blocks(NZ + 1),
            blocks(NZ + 1),
            blocks(2, 2, steps, 2),
            blocks(2, 2, steps, 2),
            blocks(2),
            blocks(2),
            dma((4,)),
            dma((2, 2, steps)),
            dma((2, 2, steps)),
            dma((2, NZ)),
            dma((2, NZ)),
            dma((n_own + n_par,)),
            dma((n_own + n_par,)),
            dma((n_own + n_par,)),
            dma((n_own + n_par,)),
            dma((2, 2)),
            dma((2, 2, steps)),
            dma((2, 2, steps)),
            dma((3,)),
        ],
        compiler_params=pltpu.CompilerParams(
            collective_id=0, has_side_effects=True, vmem_limit_bytes=60 * 2**20
        ),
    )(placement, table, live_rows, acts, grad_out, master)


def adam_update(master, moment1, moment2, gradient):
    new_moment1 = beta_first * moment1 + (1.0 - beta_first) * gradient
    new_moment2 = beta_second * moment2 + (1.0 - beta_second) * gradient * gradient
    ascent = new_moment1 / correct_first / (jnp.sqrt(new_moment2 / correct_second) + epsilon)
    new_master = master - learn_rate * (ascent + decay_rate * master)
    return (new_master, new_moment1, new_moment2)


def slot_table(placement):
    own, par, near, both = near_offsets()
    g = lax.axis_index("group")
    v = lax.axis_index("dev")
    x, y = v // NY, v % NY
    members = NX * NY
    experts = 4 * NZ
    roster = lax.dynamic_slice_in_dim(placement, g * members, members)
    other = lax.dynamic_slice_in_dim(placement, (g + 1 - 2 * (g % 2)) * members, members)
    shape = (9, experts, members)
    kind = lax.broadcasted_iota(jnp.int32, shape, 0)
    expert = lax.broadcasted_iota(jnp.int32, shape, 1)
    source = lax.broadcasted_iota(jnp.int32, shape, 2)
    dx = (x - source // NY + NX) % NX
    dy = (y - source % NY + NY + NY // 2) % NY - NY // 2
    reach = jnp.where(kind < 4, near, both)
    none = jnp.where(kind < 4, len(own), len(par))
    slot = jnp.where((dy <= reach) & (dy >= -reach), dx * (2 * reach + 1) + dy + reach, none)
    value = jnp.where(kind == 8, expert // 4, jnp.where(kind % 2 == 0, slot, -slot))
    runs = jnp.where(kind == 8, other[None, None, :], roster[None, None, :])
    match = jnp.where(kind % 4 < 2, (runs // 2 == expert // 2) & (kind < 8), False) | (runs == expert)
    best = jnp.max(jnp.where(match, value, -1000), axis=2)
    row = lax.broadcasted_iota(jnp.int32, shape[:2], 0)
    absent = jnp.where(row < 4, len(own), jnp.where(row < 8, len(par), NZ))
    return jnp.where(best == -1000, absent, jnp.abs(best))


def on_device(acts, grad_out, live_rows, placement, master, moment1, moment2):
    grad_rows, gradient = step(placement, slot_table(placement), live_rows, acts, grad_out, master)
    live_mask = (lax.iota(jnp.int32, acts.shape[0]) < live_rows[0])[:, None]
    grad_in = jnp.where(live_mask, grad_rows, jnp.zeros((), jnp.bfloat16))
    new_master, new_moment1, new_moment2 = adam_update(master, moment1, moment2, gradient)
    return (grad_in, new_master, new_moment1, new_moment2)


def solution(mesh):
    in_specs = (
        P(("group", "dev"), None),
        P(("group", "dev"), None),
        P(("group", "dev")),
        P(),
        P("group", "dev", None),
        P("group", "dev", None),
        P("group", "dev", None),
    )
    out_specs = (
        P(("group", "dev"), None),
        P("group", "dev", None),
        P("group", "dev", None),
        P("group", "dev", None),
    )
    return jax.shard_map(
        on_device, mesh=mesh, in_specs=in_specs, out_specs=out_specs, check_vma=False
    )
```

time: 139 us -> 124 us (0.89)
  the two profiles are of different devices: /device:TPU:17 before, /device:TPU:53 now
where the time goes in v2:
time: 124 us
  Pallas kernels  116 us (94%)
  other arithmetic  5.4 us (4%)
  between operations  1.42 us (1%)
    pallas_call x1, Pallas kernels, step(): pl.pallas_call(step_kernel, name='step', out_shape=(jax.ShapeDtypeStruct(...  116 us

profile of v2, /device:TPU:53, one launch (start us, length us, event | category | flops | bytes accessed | tf_op | source)
XLA Modules:
  0.0 124.1 jit_solution(9998980720748496237)
XLA Ops:
  1.3 0.8 fusion.23
  2.3 0.5 fusion.15
  2.8 0.7 abs_select_fusion.tab_ref
  3.5 0.0 copy-start
  3.5 0.0 copy-start.1
  3.5 0.0 copy-start.2
  3.5 116.4 %step.1 = (bf16[384,768]{1,0:T(8,128)(2,1)}, f32[2,24,2048]{2,1,0:T(8,128)}) custom-call(s32[512]{0:T(512)} %place_ref.1, s32[9,32]{1,0:T(8,128)} %abs_select_fusion.tab_ref, s32[1]{0:T(128)} %copy.11.live_ref, bf16[384,768]{1,0:T(8,128)(2,1)} %acts_ref.1, bf16[384,2048]{1,0:T(8,128)(2,1)} %out_ref.1, f32[2,24,2048]{2,1,0:T(8,128)} %master_ref.1), custom_call_target="tpu_custom_call" | custom-call | tf_op jit(solution)/shard_map/step/pallas_call | solution.py:374
  119.9 2.0 %broadcast_select_fusion = bf16[384,768]{1,0:T(8,128)(2,1)} fusion(bf16[384,768]{1,0:T(8,128)(2,1)} %get-tuple-element.6, pred[384]{0:T(512)(128)(4,1)S(1)} %iota_compare_fusion), kind=kLoop, calls=%fused_computation.1 | loop fusion | flops 294912 | bytes 1180032 | tf_op jit(solution)/shard_map/jit(_where)/select_n | solution.py:459
  121.9 0.0 copy-done
  121.9 0.0 copy-done.1
  121.9 0.0 copy-done.2
  121.9 2.2 %multiply_subtract_fusion = (f32[2,24,2048]{2,1,0:T(8,128)}, f32[2,24,2048]{2,1,0:T(8,128)}, f32[2,24,2048]{2,1,0:T(8,128)}) fusion(f32[2,24,2048]{2,1,0:T(8,128)S(1)} %copy-done, f32[2,24,2048]{2,1,0:T(8,128)} %get-tuple-element.7, f32[2,24,2048]{2,1,0:T(8,128)S(1)} %copy-done.1, f32[2,24,2048]{2,1,0:T(8,128)S(1)} %copy-done.2), kind=kLoop, calls=%fused_computation.8 | loop fusion | flops 1474560 | bytes 2752512 | tf_op jit(solution)/shard_map/sub | solution.py:425
  (15 shorter events, 0.1 us)
Async XLA Ops:
  3.5 118.4 %copy-start = (f32[2,24,2048]{2,1,0:T(8,128)S(1)}, f32[2,24,2048]{2,1,0:T(8,128)}, u32[]{:S(2)}) copy-start(f32[2,24,2048]{2,1,0:T(8,128)} %master_ref.1) | copy-start | bytes 1179652
  3.5 118.4 %copy-start.1 = (f32[2,24,2048]{2,1,0:T(8,128)S(1)}, f32[2,24,2048]{2,1,0:T(8,128)}, u32[]{:S(2)}) copy-start(f32[2,24,2048]{2,1,0:T(8,128)} %param.12) | copy-start | bytes 1179652
  3.5 118.4 %copy-start.2 = (f32[2,24,2048]{2,1,0:T(8,128)S(1)}, f32[2,24,2048]{2,1,0:T(8,128)}, u32[]{:S(2)}) copy-start(f32[2,24,2048]{2,1,0:T(8,128)} %param.13) | copy-start | bytes 1179652

commit v3 on v2

--- a/solution.py
+++ b/solution.py
@@ -32,11 +32,14 @@
     place_ref,
     tab_ref,
     live_ref,
+    acts_hbm,
+    out_hbm,
+    master_hbm,
+    rows_ref,
+    grad_ref,
     acts_ref,
     out_ref,
     master_ref,
-    rows_ref,
-    grad_ref,
     half_w,
     copy_g,
     weight,
@@ -98,6 +101,12 @@
             src_ref=src, dst_ref=dst, send_sem=ssem, recv_sem=rsem, device_id=dev, device_id_type=MESH
         )
 
+    fetches = [
+        pltpu.make_async_copy(src, dst, local_sem.at[3 + i])
+        for i, (src, dst) in enumerate(((master_hbm, master_ref), (acts_hbm, acts_ref), (out_hbm, out_ref)))
+    ]
+    for cp in fetches:
+        cp.start()
     barrier = pltpu.get_barrier_semaphore()
     peers = [(g, at(dx, dy)) for dx, dy in own if (dx, dy) != (0, 0)] + [pair_dev, core_dev]
     if NZ > 1:
@@ -105,12 +114,13 @@
     for dev in peers:
         pl.semaphore_signal(barrier, inc=1, device_id=dev, device_id_type=MESH)
 
-    half_w[...] = master_ref[...].astype(jnp.bfloat16)
     zero = jnp.zeros((rows, width), jnp.bfloat16)
     g_own[n_own] = zero
     g_par[n_par] = zero
     d_own[NZ] = zero
     d_par[NZ] = zero
+    fetches[0].wait()
+    half_w[...] = master_ref[...].astype(jnp.bfloat16)
     pl.semaphore_wait(barrier, len(peers))
 
     sends = []
@@ -178,6 +188,8 @@
     local_w = pltpu.make_async_copy(half_w, w_all[0].at[block], local_sem.at[0])
     local_w.start()
 
+    fetches[1].wait()
+    fetches[2].wait()
     live = lax.broadcasted_iota(jnp.int32, acts_ref.shape, 0) < live_ref[0]
     masked = jnp.where(live, acts_ref[...], jnp.zeros((), jnp.bfloat16))
     strip = min(512, width)
@@ -340,18 +352,21 @@
     for step in range(2, steps + 1):
         rs_step(0, step)
     rs_last(0)
-    back.wait_recv()
-    for j in (0, 1):
-        grad_ref[j] = home_sum(0, j) + p_recv[j].astype(jnp.float32)
-
-    for dx in sorted(range(NX), key=lambda d: (min(d, NX - d), d)):
+
+    kept = lax.broadcasted_iota(jnp.int32, (acts_ref.shape[0], NY * rows), 0) < live_ref[0]
+    for i, dx in enumerate(sorted(range(NX), key=lambda d: (min(d, NX - d), d))):
+        if i == NX - 1:
+            back.wait_recv()
+            for j in (0, 1):
+                grad_ref[j] = home_sum(0, j) + p_recv[j].astype(jnp.float32)
         for cp in w_waits.get(dx, []):
             cp.wait_recv()
         xs = lax.rem(x - dx + NX, NX)
         part = weight[pl.ds(xs * NY, NY)].reshape(NY * rows, width)
-        in_parts[xs] = lax.dot_general(
+        product = lax.dot_general(
             out_ref[...], part, (((1,), (1,)), ((), ())), preferred_element_type=jnp.float32
-        ).astype(jnp.bfloat16)
+        )
+        in_parts[xs] = jnp.where(kept, product, jnp.zeros((), jnp.float32)).astype(jnp.bfloat16)
     for xs in range(NX):
         rows_ref[:, xs * NY * rows : (xs + 1) * NY * rows] = in_parts[xs]
     for cp in sends:
@@ -367,6 +382,7 @@
     dma = pltpu.SemaphoreType.DMA
     vmem = pl.BlockSpec(memory_space=pltpu.VMEM)
     smem = pl.BlockSpec(memory_space=pltpu.SMEM)
+    anywhere = pl.BlockSpec(memory_space=pl.ANY)
 
     def blocks(*lead):
         return pltpu.VMEM(lead + (rows, width), jnp.bfloat16)
@@ -378,9 +394,12 @@
             jax.ShapeDtypeStruct(acts.shape, jnp.bfloat16),
             jax.ShapeDtypeStruct(master.shape, jnp.float32),
         ),
-        in_specs=[smem, smem, smem, vmem, vmem, vmem],
+        in_specs=[smem, smem, smem, anywhere, anywhere, anywhere],
         out_specs=(vmem, vmem),
         scratch_shapes=[
+            pltpu.VMEM(acts.shape, acts.dtype),
+            pltpu.VMEM(grad_out.shape, grad_out.dtype),
+            pltpu.VMEM(master.shape, master.dtype),
             blocks(2),
             blocks(NX * NY),
             blocks(NX * NY),
@@ -410,7 +429,7 @@
             dma((2, 2)),
             dma((2, 2, steps)),
             dma((2, 2, steps)),
-            dma((3,)),
+            dma((6,)),
         ],
         compiler_params=pltpu.CompilerParams(
             collective_id=0, has_side_effects=True, vmem_limit_bytes=60 * 2**20
@@ -454,9 +473,7 @@
 
 
 def on_device(acts, grad_out, live_rows, placement, master, moment1, moment2):
-    grad_rows, gradient = step(placement, slot_table(placement), live_rows, acts, grad_out, master)
-    live_mask = (lax.iota(jnp.int32, acts.shape[0]) < live_rows[0])[:, None]
-    grad_in = jnp.where(live_mask, grad_rows, jnp.zeros((), jnp.bfloat16))
+    grad_in, gradient = step(placement, slot_table(placement), live_rows, acts, grad_out, master)
     new_master, new_moment1, new_moment2 = adam_update(master, moment1, moment2, gradient)
     return (grad_in, new_master, new_moment1, new_moment2)
 

time: 124 us -> 120 us (0.968)
  the two profiles are of different devices: /device:TPU:53 before, /device:TPU:47 now
where the time goes in v3:
time: 120 us
  Pallas kernels  113 us (94%)
  other arithmetic  3.45 us (3%)
  local copies, waits for them, and re-layouts  1.67 us (1%)
  between operations  1.55 us (1%)
    pallas_call x1, Pallas kernels, step(): pl.pallas_call(step_kernel, name='step', out_shape=(jax.ShapeDtypeStruct(...  113 us

profile of v3, /device:TPU:47, one launch (start us, length us, event | category | flops | bytes accessed | tf_op | source)
XLA Modules:
  0.0 120.0 jit_solution(1705550532957568022)
XLA Ops:
  0.6 0.0 copy-start
  0.6 0.0 copy-start.3
  0.7 0.0 copy-start.2
  1.4 0.8 fusion.23
  2.4 0.5 fusion.15
  2.9 0.7 abs_select_fusion.tab_ref
  3.6 113.3 %step.1 = (bf16[384,768]{1,0:T(8,128)(2,1)}, f32[2,24,2048]{2,1,0:T(8,128)}) custom-call(s32[512]{0:T(512)} %place_ref.1, s32[9,32]{1,0:T(8,128)} %abs_select_fusion.tab_ref, s32[1]{0:T(128)S(6)} %copy.12.live_ref, bf16[384,768]{1,0:T(8,128)(2,1)} %acts_hbm.1, bf16[384,2048]{1,0:T(8,128)(2,1)} %out_hbm.1, f32[2,24,2048]{2,1,0:T(8,128)} %master_hbm.1), custom_call_target="tpu_custom_call" | custom-call | tf_op jit(solution)/shard_map/step/pallas_call | solution.py:390
  116.9 0.0 copy-start.1
  116.9 0.0 copy-done
  116.9 0.0 copy-done.3
  116.9 0.0 copy-done.2
  116.9 2.2 %multiply_subtract_fusion = (f32[2,24,2048]{2,1,0:T(8,128)}, f32[2,24,2048]{2,1,0:T(8,128)}, f32[2,24,2048]{2,1,0:T(8,128)}) fusion(f32[2,24,2048]{2,1,0:T(8,128)S(1)} %copy-done, f32[2,24,2048]{2,1,0:T(8,128)} %get-tuple-element.7, f32[2,24,2048]{2,1,0:T(8,128)S(1)} %copy-done.2, f32[2,24,2048]{2,1,0:T(8,128)S(1)} %copy-done.3), kind=kLoop, calls=%fused_computation.7 | loop fusion | flops 1474560 | bytes 2752512 | tf_op jit(solution)/shard_map/sub | solution.py:444
  119.2 0.0 copy-done.1
  119.2 0.8 copy.13
  (14 shorter events, 0.1 us)
Async XLA Ops:
  0.6 116.3 %copy-start = (f32[2,24,2048]{2,1,0:T(8,128)S(1)}, f32[2,24,2048]{2,1,0:T(8,128)}, u32[]{:S(2)}) copy-start(f32[2,24,2048]{2,1,0:T(8,128)} %master_hbm.1) | copy-start | bytes 1179652
  0.6 116.3 %copy-start.3 = (f32[2,24,2048]{2,1,0:T(8,128)S(1)}, f32[2,24,2048]{2,1,0:T(8,128)}, u32[]{:S(2)}) copy-start(f32[2,24,2048]{2,1,0:T(8,128)} %param.13) | copy-start | bytes 1179652
  0.7 116.3 %copy-start.2 = (f32[2,24,2048]{2,1,0:T(8,128)S(1)}, f32[2,24,2048]{2,1,0:T(8,128)}, u32[]{:S(2)}) copy-start(f32[2,24,2048]{2,1,0:T(8,128)} %param.12) | copy-start | bytes 1179652
  116.9 2.3 %copy-start.1 = (bf16[384,768]{1,0:T(8,128)(2,1)S(1)}, bf16[384,768]{1,0:T(8,128)(2,1)}, u32[]{:S(2)}) copy-start(bf16[384,768]{1,0:T(8,128)(2,1)} %get-tuple-element.41) | copy-start | bytes 1769476

commit v4 on v3

--- a/solution.py
+++ b/solution.py
@@ -19,24 +19,32 @@
 NX, NY, NZ = 4, 8, 8
 
 
-def near_offsets():
-    half = NY // 2
-    near = half // 2
-    both = (half - 1) // 2
-    own = [(dx, dy) for dx in range(NX) for dy in range(-near, near + 1)]
-    par = [(dx, dy) for dx in range(NX) for dy in range(-both, both + 1)]
-    return own, par, near, both
+SKIP = 3
+SPAN = 4
+W_LOW = (-1, -2)
+G_LOW = (-2, -1)
+
+
+def offsets(low):
+    return [(dx, dy) for dx in range(NX) for dy in range(low, low + SPAN)]
+
+
+def by_distance(places):
+    far = sorted(places, key=lambda d: (-(min(d[0], NX - d[0]) + abs(d[1])), d))
+    return [d for d in far if d != (0, 0)]
 
 
 def step_kernel(
     place_ref,
-    tab_ref,
+    place_vec,
     live_ref,
     acts_hbm,
     out_hbm,
     master_hbm,
     rows_ref,
     grad_ref,
+    tab_vec,
+    tab_ref,
     acts_ref,
     out_ref,
     master_ref,
@@ -75,10 +83,9 @@
     v = lax.axis_index("dev")
     z, c = g // 2, g % 2
     x, y = v // NY, v % NY
-    half = NY // 2
-    own, par, near, both = near_offsets()
-    n_own, n_par = len(own), len(par)
-    vp = x * NY + lax.rem(y + half, NY)
+    w_places, g_places = [offsets(low) for low in W_LOW], [offsets(low) for low in G_LOW]
+    slots = NX * SPAN
+    vp = x * NY + lax.rem(y + SKIP, NY)
     members = NX * NY
     rows, width = half_w.shape[1:]
     w_all, d_recv = (w_own, w_par), (d_own, d_par)
@@ -86,13 +93,14 @@
     def at(dx, dy):
         return lax.rem(x + dx + NX, NX) * NY + lax.rem(y + dy + NY, NY)
 
-    def pair_of(vd):
-        return (vd // NY) * NY + lax.rem(vd % NY + half, NY)
+    def held_by(vd):
+        return (vd // NY) * NY + lax.rem(vd % NY + SKIP, NY)
 
     def zmod(k):
         return lax.rem(z + k + NZ, NZ)
 
-    pair_dev = (g, vp)
+    up_dev = (g, vp)
+    down_dev = (g, x * NY + lax.rem(y + NY - SKIP, NY))
     core_dev = (z * 2 + 1 - c, v)
     z_dev = ((zmod(1) * 2 + c, v), (zmod(-1) * 2 + c, v))
 
@@ -108,19 +116,70 @@
     for cp in fetches:
         cp.start()
     barrier = pltpu.get_barrier_semaphore()
-    peers = [(g, at(dx, dy)) for dx, dy in own if (dx, dy) != (0, 0)] + [pair_dev, core_dev]
+    near = sorted(set(w_places[0] + w_places[1] + g_places[0] + g_places[1]) - {(0, 0)})
+    peers = [(g, at(dx, dy)) for dx, dy in near] + [up_dev, down_dev, core_dev]
     if NZ > 1:
         peers += list(z_dev)
     for dev in peers:
         pl.semaphore_signal(barrier, inc=1, device_id=dev, device_id_type=MESH)
 
     zero = jnp.zeros((rows, width), jnp.bfloat16)
-    g_own[n_own] = zero
-    g_par[n_par] = zero
+    g_own[slots] = zero
+    g_par[slots] = zero
     d_own[NZ] = zero
     d_par[NZ] = zero
+    lanes = place_vec.shape[1]
+    groups_per_row = lanes // members
+    everyone = place_vec[pl.ds(g // groups_per_row, 1), :]
+    shape = (4 * NZ, lanes)
+    experts = lax.broadcasted_iota(jnp.int32, shape, 0)
+    lane = lax.broadcasted_iota(jnp.int32, shape, 1)
+    runs = jnp.broadcast_to(everyone, shape)
+    place_of = lax.rem(g, groups_per_row) * members
+    other_of = lax.rem(z * 2 + 1 - c, groups_per_row) * members
+    in_group = (lane >= place_of) & (lane < place_of + members)
+    in_other = (lane >= other_of) & (lane < other_of + members)
+    source = lane & (members - 1)
+    dx = (x - source // NY + NX) & (NX - 1)
+    dy = ((y - (source & (NY - 1)) + NY // 2) & (NY - 1)) - NY // 2
+    same_owner = in_group & ((runs >> 1) == (experts >> 1))
+    same_expert = in_group & (runs == experts)
+    column = lax.broadcasted_iota(jnp.int32, tab_vec.shape, 1)
+    table = jnp.zeros(tab_vec.shape, jnp.int32)
+
+    def put(table, k, match, value, absent):
+        best = jnp.max(jnp.where(match, value, -1000), axis=1, keepdims=True)
+        best = jnp.where(best == -1000, absent, jnp.abs(best))
+        return jnp.where(column == k, best, table)
+
+    for h in (0, 1):
+        inside = (dy >= G_LOW[h]) & (dy < G_LOW[h] + SPAN)
+        slot = jnp.where(inside, dx * SPAN + dy - G_LOW[h], slots)
+        table = put(table, 4 * h, same_owner, slot, slots)
+        table = put(table, 4 * h + 1, same_owner, -slot, slots)
+        table = put(table, 4 * h + 2, same_expert, slot, slots)
+        table = put(table, 4 * h + 3, same_expert, -slot, slots)
+    table = put(table, 8, in_other & (runs == experts), experts >> 2, NZ)
+    tab_vec[...] = table
+
     fetches[0].wait()
     half_w[...] = master_ref[...].astype(jnp.bfloat16)
+    fetches[1].wait()
+    fetches[2].wait()
+    live = lax.broadcasted_iota(jnp.int32, acts_ref.shape, 0) < live_ref[0]
+    masked = jnp.where(live, acts_ref[...], jnp.zeros((), jnp.bfloat16))
+    strip = min(512, width)
+
+    def copy_strip(i, carry):
+        cols = pl.ds(pl.multiple_of(i * strip, strip), strip)
+        product = lax.dot_general(
+            masked, out_ref[:, cols], (((0,), (0,)), ((), ())), preferred_element_type=jnp.float32
+        )
+        copy_g[:, :, cols] = product.astype(jnp.bfloat16).reshape(members, rows, strip)
+        return carry
+
+    early_strips = width // strip // 2
+    lax.fori_loop(0, early_strips, copy_strip, 0)
     pl.semaphore_wait(barrier, len(peers))
 
     sends = []
@@ -130,7 +189,7 @@
         sends.append(cp)
 
     block = pl.ds(2 * g, 2)
-    pair_copy = remote(half_w, w_all[1].at[block], pair_sem.at[0], pair_sem.at[1], pair_dev)
+    pair_copy = remote(half_w, w_all[1].at[block], pair_sem.at[0], pair_sem.at[1], down_dev)
     go(pair_copy)
     hops = ((NZ // 2, (NZ - 1) // 2), ((NZ - 1) // 2, NZ // 2))
 
@@ -187,26 +246,14 @@
     launch(0, half_w)
     local_w = pltpu.make_async_copy(half_w, w_all[0].at[block], local_sem.at[0])
     local_w.start()
-
-    fetches[1].wait()
-    fetches[2].wait()
-    live = lax.broadcasted_iota(jnp.int32, acts_ref.shape, 0) < live_ref[0]
-    masked = jnp.where(live, acts_ref[...], jnp.zeros((), jnp.bfloat16))
-    strip = min(512, width)
-
-    def copy_strip(i, carry):
-        cols = pl.ds(pl.multiple_of(i * strip, strip), strip)
-        product = lax.dot_general(
-            masked, out_ref[:, cols], (((0,), (0,)), ((), ())), preferred_element_type=jnp.float32
-        )
-        copy_g[:, :, cols] = product.astype(jnp.bfloat16).reshape(members, rows, strip)
-        return carry
-
-    lax.fori_loop(0, width // strip, copy_strip, 0)
+    table_copy = pltpu.make_async_copy(tab_vec, tab_ref, local_sem.at[6])
+    table_copy.start()
+
+    lax.fori_loop(early_strips, width // strip, copy_strip, 0)
 
     local_g = [
-        pltpu.make_async_copy(copy_g.at[v], g_own.at[own.index((0, 0))], local_sem.at[1]),
-        pltpu.make_async_copy(copy_g.at[vp], g_par.at[par.index((0, 0))], local_sem.at[2]),
+        pltpu.make_async_copy(copy_g.at[v], g_own.at[g_places[0].index((0, 0))], local_sem.at[1]),
+        pltpu.make_async_copy(copy_g.at[vp], g_par.at[g_places[1].index((0, 0))], local_sem.at[2]),
     ]
     for cp in local_g:
         cp.start()
@@ -217,16 +264,13 @@
         go(cp)
         g_waits[h].append(cp)
 
-    order = sorted(own, key=lambda d: (-(min(d[0], NX - d[0]) + abs(d[1])), d))
-    order = [d for d in order if d != (0, 0)]
-    for dx, dy in order:
-        if (dx, dy) in par:
-            vd = at(dx, dy)
-            s = par.index((dx, dy))
-            g_go(1, copy_g.at[pair_of(vd)], g_par.at[s], n_own + s, (g, vd))
-    for dx, dy in order:
+    for dx, dy in by_distance(g_places[1]):
         vd = at(dx, dy)
-        s = own.index((dx, dy))
+        s = g_places[1].index((dx, dy))
+        g_go(1, copy_g.at[held_by(vd)], g_par.at[s], slots + s, (g, vd))
+    for dx, dy in by_distance(g_places[0]):
+        vd = at(dx, dy)
+        s = g_places[0].index((dx, dy))
         g_go(0, copy_g.at[vd], g_own.at[s], s, (g, vd))
 
     w_waits = {}
@@ -236,22 +280,16 @@
         go(cp)
         w_waits.setdefault(dx, []).append(cp)
 
-    def deal_own():
-        for dx, dy in order:
+    w_send = (w_send_own, w_send_par)
+
+    def deal(h):
+        home = vp if h else v
+        for dx, dy in by_distance(w_places[h]):
             vd = at(dx, dy)
-            s = own.index((dx, dy))
-            w_send_own[s] = w_all[0][place_ref[g * members + vd]]
-            w_go(w_send_own.at[s], weight.at[v], s, (g, vd), dx)
-        weight[v] = w_all[0][place_ref[g * members + v]]
-
-    def deal_par():
-        for dx, dy in order:
-            if (dx, dy) in par:
-                vd = at(dx, dy)
-                s = par.index((dx, dy))
-                w_send_par[s] = w_all[1][place_ref[g * members + vd]]
-                w_go(w_send_par.at[s], weight.at[vp], n_own + s, (g, vd), dx)
-        weight[vp] = w_all[1][place_ref[g * members + v]]
+            s = w_places[h].index((dx, dy))
+            w_send[h][s] = w_all[h][place_ref[g * members + vd]]
+            w_go(w_send[h].at[s], weight.at[home], h * slots + s, (g, vd), dx)
+        weight[home] = w_all[h][place_ref[g * members + v]]
 
     recv = (g_own, g_par)
 
@@ -265,8 +303,8 @@
 
         def owner_sum(zz, carry):
             e = 2 * (2 * zz + 1 - c)
-            first = recv[h][tab_ref[4 * h, e]].astype(jnp.float32)
-            second = recv[h][tab_ref[4 * h + 1, e]].astype(jnp.float32)
+            first = recv[h][tab_ref[e, 4 * h]].astype(jnp.float32)
+            second = recv[h][tab_ref[e, 4 * h + 1]].astype(jnp.float32)
             d_send[h, zz] = (first + second).astype(jnp.bfloat16)
             return carry
 
@@ -275,9 +313,9 @@
 
     def chip_sum(h, zt, j):
         e = 2 * (2 * zt + c) + j
-        first = recv[h][tab_ref[4 * h + 2, e]].astype(jnp.float32)
-        second = recv[h][tab_ref[4 * h + 3, e]].astype(jnp.float32)
-        return first + second + d_recv[h][tab_ref[8, e]].astype(jnp.float32)
+        first = recv[h][tab_ref[e, 4 * h + 2]].astype(jnp.float32)
+        second = recv[h][tab_ref[e, 4 * h + 3]].astype(jnp.float32)
+        return first + second + d_recv[h][tab_ref[e, 8]].astype(jnp.float32)
 
     def rs(h, way, step):
         return remote(
@@ -323,6 +361,7 @@
     launch(1, None)
     forward(0, 3)
     forward(1, 1)
+    table_copy.wait()
     give_core(1)
     for k in range(4, steps + 1):
         forward(0, k)
@@ -331,23 +370,23 @@
     rs_step(1, 1)
     local_w.wait()
     core_arrived(0)
-    deal_own()
+    deal(0)
     forward(1, 3)
     rs_step(1, 2)
     for k in range(4, steps + 1):
         forward(1, k)
     core_arrived(1)
-    deal_par()
+    deal(1)
     rs_step(1, 3)
     give_core(0)
+    core_swap(0).wait_recv()
+    rs_step(0, 1)
     for step in range(4, steps + 1):
         rs_step(1, step)
-    core_swap(0).wait_recv()
-    rs_step(0, 1)
     rs_last(1)
     for j in (0, 1):
         p_send[j] = home_sum(1, j).astype(jnp.bfloat16)
-    back = remote(p_send, p_recv, pair_sem.at[2], pair_sem.at[3], pair_dev)
+    back = remote(p_send, p_recv, pair_sem.at[2], pair_sem.at[3], up_dev)
     go(back)
     for step in range(2, steps + 1):
         rs_step(0, step)
@@ -373,10 +412,10 @@
         cp.wait_send()
 
 
-def step(placement, table, live_rows, acts, grad_out, master):
+def step(placement, live_rows, acts, grad_out, master):
     rows, width = master.shape[1:]
-    own, par, _, _ = near_offsets()
-    n_own, n_par = len(own), len(par)
+    slots = NX * SPAN
+    lanes = min(128, placement.shape[0])
     owners = 2 * NZ
     steps = max(1, NZ // 2)
     dma = pltpu.SemaphoreType.DMA
@@ -394,9 +433,11 @@
             jax.ShapeDtypeStruct(acts.shape, jnp.bfloat16),
             jax.ShapeDtypeStruct(master.shape, jnp.float32),
         ),
-        in_specs=[smem, smem, smem, anywhere, anywhere, anywhere],
+        in_specs=[smem, vmem, smem, anywhere, anywhere, anywhere],
         out_specs=(vmem, vmem),
         scratch_shapes=[
+            pltpu.VMEM((2 * owners, 128), jnp.int32),
+            pltpu.SMEM((2 * owners, 128), jnp.int32),
             pltpu.VMEM(acts.shape, acts.dtype),
             pltpu.VMEM(grad_out.shape, grad_out.dtype),
             pltpu.VMEM(master.shape, master.dtype),
@@ -406,10 +447,10 @@
             pltpu.VMEM((NX, acts.shape[0], NY * rows), jnp.bfloat16),
             blocks(2 * owners),
             blocks(2 * owners),
-            blocks(n_own),
-            blocks(n_par),
-            blocks(n_own + 1),
-            blocks(n_par + 1),
+            blocks(slots),
+            blocks(slots),
+            blocks(slots + 1),
+            blocks(slots + 1),
             blocks(2, NZ),
             blocks(NZ + 1),
             blocks(NZ + 1),
@@ -422,58 +463,32 @@
             dma((2, 2, steps)),
             dma((2, NZ)),
             dma((2, NZ)),
-            dma((n_own + n_par,)),
-            dma((n_own + n_par,)),
-            dma((n_own + n_par,)),
-            dma((n_own + n_par,)),
+            dma((2 * slots,)),
+            dma((2 * slots,)),
+            dma((2 * slots,)),
+            dma((2 * slots,)),
             dma((2, 2)),
             dma((2, 2, steps)),
             dma((2, 2, steps)),
-            dma((6,)),
+            dma((7,)),
         ],
         compiler_params=pltpu.CompilerParams(
             collective_id=0, has_side_effects=True, vmem_limit_bytes=60 * 2**20
         ),
-    )(placement, table, live_rows, acts, grad_out, master)
+    )(placement, placement.reshape(-1, lanes), live_rows, acts, grad_out, master)
 
 
 def adam_update(master, moment1, moment2, gradient):
     new_moment1 = beta_first * moment1 + (1.0 - beta_first) * gradient
     new_moment2 = beta_second * moment2 + (1.0 - beta_second) * gradient * gradient
-    ascent = new_moment1 / correct_first / (jnp.sqrt(new_moment2 / correct_second) + epsilon)
+    root = jnp.sqrt(new_moment2 * (correct_first**2 / correct_second))
+    ascent = new_moment1 / (root + correct_first * epsilon)
     new_master = master - learn_rate * (ascent + decay_rate * master)
     return (new_master, new_moment1, new_moment2)
 
 
-def slot_table(placement):
-    own, par, near, both = near_offsets()
-    g = lax.axis_index("group")
-    v = lax.axis_index("dev")
-    x, y = v // NY, v % NY
-    members = NX * NY
-    experts = 4 * NZ
-    roster = lax.dynamic_slice_in_dim(placement, g * members, members)
-    other = lax.dynamic_slice_in_dim(placement, (g + 1 - 2 * (g % 2)) * members, members)
-    shape = (9, experts, members)
-    kind = lax.broadcasted_iota(jnp.int32, shape, 0)
-    expert = lax.broadcasted_iota(jnp.int32, shape, 1)
-    source = lax.broadcasted_iota(jnp.int32, shape, 2)
-    dx = (x - source // NY + NX) % NX
-    dy = (y - source % NY + NY + NY // 2) % NY - NY // 2
-    reach = jnp.where(kind < 4, near, both)
-    none = jnp.where(kind < 4, len(own), len(par))
-    slot = jnp.where((dy <= reach) & (dy >= -reach), dx * (2 * reach + 1) + dy + reach, none)
-    value = jnp.where(kind == 8, expert // 4, jnp.where(kind % 2 == 0, slot, -slot))
-    runs = jnp.where(kind == 8, other[None, None, :], roster[None, None, :])
-    match = jnp.where(kind % 4 < 2, (runs // 2 == expert // 2) & (kind < 8), False) | (runs == expert)
-    best = jnp.max(jnp.where(match, value, -1000), axis=2)
-    row = lax.broadcasted_iota(jnp.int32, shape[:2], 0)
-    absent = jnp.where(row < 4, len(own), jnp.where(row < 8, len(par), NZ))
-    return jnp.where(best == -1000, absent, jnp.abs(best))
-
-
 def on_device(acts, grad_out, live_rows, placement, master, moment1, moment2):
-    grad_in, gradient = step(placement, slot_table(placement), live_rows, acts, grad_out, master)
+    grad_in, gradient = step(placement, live_rows, acts, grad_out, master)
     new_master, new_moment1, new_moment2 = adam_update(master, moment1, moment2, gradient)
     return (grad_in, new_master, new_moment1, new_moment2)
 

time: 120 us -> 111 us (0.925)
  the two profiles are of different devices: /device:TPU:47 before, /device:TPU:44 now
where the time goes in v4:
time: 111 us
  Pallas kernels  106 us (95%)
  other arithmetic  2.22 us (2%)
  between operations  1.43 us (1%)
    pallas_call x1, Pallas kernels, step(): pl.pallas_call(step_kernel, name='step', out_shape=(jax.ShapeDtypeStruct(...  106 us
    sub x1, other arithmetic, adam_update(): new_master = master - learn_rate * (ascent + decay_rate * master)  2.22 us

profile of v4, /device:TPU:44, one launch (start us, length us, event | category | flops | bytes accessed | tf_op | source)
XLA Modules:
  0.0 110.8 jit_solution(16905765400922708015)
XLA Ops:
  0.6 0.0 copy-start
  0.6 0.0 copy-start.2
  0.7 0.0 copy-start.3
  1.4 106.3 %step.1 = (bf16[384,768]{1,0:T(8,128)(2,1)}, f32[2,24,2048]{2,1,0:T(8,128)}) custom-call(s32[512]{0:T(512)} %place_ref.1, s32[4,128]{1,0:T(4,128)} %bitcast.1, s32[1]{0:T(128)S(6)} %copy.12.live_ref, bf16[384,768]{1,0:T(8,128)(2,1)} %acts_hbm.1, bf16[384,2048]{1,0:T(8,128)(2,1)} %out_hbm.1, f32[2,24,2048]{2,1,0:T(8,128)} %master_hbm.1), custom_call_target="tpu_custom_call" | custom-call | tf_op jit(solution)/shard_map/step/pallas_call | solution.py:429
  107.7 0.0 copy-start.1
  107.8 0.0 copy-done
  107.8 0.0 copy-done.2
  107.8 0.0 copy-done.3
  107.8 2.2 %multiply_subtract_fusion = (f32[2,24,2048]{2,1,0:T(8,128)}, f32[2,24,2048]{2,1,0:T(8,128)}, f32[2,24,2048]{2,1,0:T(8,128)}) fusion(f32[2,24,2048]{2,1,0:T(8,128)S(1)} %copy-done, f32[2,24,2048]{2,1,0:T(8,128)} %get-tuple-element.7, f32[2,24,2048]{2,1,0:T(8,128)S(1)} %copy-done.2, f32[2,24,2048]{2,1,0:T(8,128)S(1)} %copy-done.3), kind=kLoop, calls=%fused_computation.2 | loop fusion | flops 1376256 | bytes 2752512 | tf_op jit(solution)/shard_map/sub | solution.py:486
  110.0 0.0 copy-done.1
  110.0 0.8 copy.13
Async XLA Ops:
  0.6 107.1 %copy-start = (f32[2,24,2048]{2,1,0:T(8,128)S(1)}, f32[2,24,2048]{2,1,0:T(8,128)}, u32[]{:S(2)}) copy-start(f32[2,24,2048]{2,1,0:T(8,128)} %master_hbm.1) | copy-start | bytes 1179652
  0.6 107.1 %copy-start.2 = (f32[2,24,2048]{2,1,0:T(8,128)S(1)}, f32[2,24,2048]{2,1,0:T(8,128)}, u32[]{:S(2)}) copy-start(f32[2,24,2048]{2,1,0:T(8,128)} %param.13) | copy-start | bytes 1179652
  0.7 107.1 %copy-start.3 = (f32[2,24,2048]{2,1,0:T(8,128)S(1)}, f32[2,24,2048]{2,1,0:T(8,128)}, u32[]{:S(2)}) copy-start(f32[2,24,2048]{2,1,0:T(8,128)} %param.12) | copy-start | bytes 1179652
  107.7 2.3 %copy-start.1 = (bf16[384,768]{1,0:T(8,128)(2,1)S(1)}, bf16[384,768]{1,0:T(8,128)(2,1)}, u32[]{:S(2)}) copy-start(bf16[384,768]{1,0:T(8,128)(2,1)} %get-tuple-element.15) | copy-start | bytes 1769476

commit v5 on v4

--- a/solution.py
+++ b/solution.py
@@ -30,7 +30,7 @@
 
 
 def by_distance(places):
-    far = sorted(places, key=lambda d: (-(min(d[0], NX - d[0]) + abs(d[1])), d))
+    far = sorted(places, key=lambda d: (-min(d[0], NX - d[0]), abs(d[1]), d[1], d[0]))
     return [d for d in far if d != (0, 0)]
 
 
@@ -193,23 +193,24 @@
     go(pair_copy)
     hops = ((NZ // 2, (NZ - 1) // 2), ((NZ - 1) // 2, NZ // 2))
 
-    def ag(ring, way, step, src=None):
+    def ag(ring, way, step, j, src=None):
         k = step - 1
         o = zmod(-k if way == 0 else k) * 2 + c
-        part = w_all[ring].at[pl.ds(2 * o, 2)]
+        part = w_all[ring].at[2 * o + j]
         return remote(
-            part if src is None else src,
+            part if src is None else src.at[j],
             part,
-            ag_send_sem.at[ring, way, k],
-            ag_recv_sem.at[ring, way, k],
+            ag_send_sem.at[ring, way, k, j],
+            ag_recv_sem.at[ring, way, k, j],
             z_dev[way],
         )
 
-    def ag_arrived(ring, way, step):
+    def ag_arrived(ring, way, step, j):
         o = zmod(-step if way == 0 else step) * 2 + c
-        part = w_all[ring].at[pl.ds(2 * o, 2)]
+        part = w_all[ring].at[2 * o + j]
+        k = step - 1
         remote(
-            part, part, ag_send_sem.at[ring, way, step - 1], ag_recv_sem.at[ring, way, step - 1], z_dev[way]
+            part, part, ag_send_sem.at[ring, way, k, j], ag_recv_sem.at[ring, way, k, j], z_dev[way]
         ).wait_recv()
 
     def core_copy(ring, k, src=None):
@@ -230,18 +231,21 @@
             remote(part, part, core_send_sem.at[ring, k], core_recv_sem.at[ring, k], core_dev).wait_recv()
 
     def launch(ring, src):
-        for way in (0, 1):
-            if hops[ring][way] > 0:
-                go(ag(ring, way, 1, src))
+        for j in (0, 1):
+            for way in (0, 1):
+                if hops[ring][way] > 0:
+                    go(ag(ring, way, 1, j, src))
         go(core_copy(ring, 0, src))
 
     def forward(ring, step):
-        for way in (0, 1):
-            if 1 <= step <= hops[ring][way]:
-                ag_arrived(ring, way, step)
+        ways = [way for way in (0, 1) if 1 <= step <= hops[ring][way]]
+        for j in (0, 1):
+            for way in ways:
+                ag_arrived(ring, way, step, j)
                 if step < hops[ring][way]:
-                    go(ag(ring, way, step + 1))
-                go(core_copy(ring, step if way == 0 else NZ - step))
+                    go(ag(ring, way, step + 1, j))
+        for way in ways:
+            go(core_copy(ring, step if way == 0 else NZ - step))
 
     launch(0, half_w)
     local_w = pltpu.make_async_copy(half_w, w_all[0].at[block], local_sem.at[0])
@@ -317,35 +321,36 @@
         second = recv[h][tab_ref[e, 4 * h + 3]].astype(jnp.float32)
         return first + second + d_recv[h][tab_ref[e, 8]].astype(jnp.float32)
 
-    def rs(h, way, step):
+    def rs(h, way, step, j):
         return remote(
-            r_send.at[h, way, step - 1],
-            r_recv.at[h, way, step - 1],
-            rs_send_sem.at[h, way, step - 1],
-            rs_recv_sem.at[h, way, step - 1],
+            r_send.at[h, way, step - 1, j],
+            r_recv.at[h, way, step - 1, j],
+            rs_send_sem.at[h, way, step - 1, j],
+            rs_recv_sem.at[h, way, step - 1, j],
             z_dev[1 - way],
         )
 
     def rs_step(h, step):
-        for way in (0, 1):
-            length = hops[h][way]
-            if step > length:
-                continue
-            away = length - step + 1
-            zt = zmod(-away if way == 0 else away)
-            if step > 1:
-                rs(h, way, step - 1).wait_recv()
-            for j in (0, 1):
+        for j in (0, 1):
+            for way in (0, 1):
+                length = hops[h][way]
+                if step > length:
+                    continue
+                away = length - step + 1
+                zt = zmod(-away if way == 0 else away)
+                if step > 1:
+                    rs(h, way, step - 1, j).wait_recv()
                 total = chip_sum(h, zt, j)
                 if step > 1:
                     total = total + r_recv[h, way, step - 2, j].astype(jnp.float32)
                 r_send[h, way, step - 1, j] = total.astype(jnp.bfloat16)
-            go(rs(h, way, step))
+                go(rs(h, way, step, j))
 
     def rs_last(h):
-        for way in (0, 1):
-            if hops[h][way] > 0:
-                rs(h, way, hops[h][way]).wait_recv()
+        for j in (0, 1):
+            for way in (0, 1):
+                if hops[h][way] > 0:
+                    rs(h, way, hops[h][way], j).wait_recv()
 
     def home_sum(h, j):
         total = chip_sum(h, z, j)
@@ -383,18 +388,20 @@
     rs_step(0, 1)
     for step in range(4, steps + 1):
         rs_step(1, step)
+    if steps > 1:
+        rs_step(0, 2)
     rs_last(1)
     for j in (0, 1):
         p_send[j] = home_sum(1, j).astype(jnp.bfloat16)
     back = remote(p_send, p_recv, pair_sem.at[2], pair_sem.at[3], up_dev)
     go(back)
-    for step in range(2, steps + 1):
+    for step in range(3, steps + 1):
         rs_step(0, step)
-    rs_last(0)
 
     kept = lax.broadcasted_iota(jnp.int32, (acts_ref.shape[0], NY * rows), 0) < live_ref[0]
-    for i, dx in enumerate(sorted(range(NX), key=lambda d: (min(d, NX - d), d))):
+    for i, dx in enumerate(sorted(range(NX), key=lambda d: (-min(d, NX - d), d))):
         if i == NX - 1:
+            rs_last(0)
             back.wait_recv()
             for j in (0, 1):
                 grad_ref[j] = home_sum(0, j) + p_recv[j].astype(jnp.float32)
@@ -459,8 +466,8 @@
             blocks(2),
             blocks(2),
             dma((4,)),
-            dma((2, 2, steps)),
-            dma((2, 2, steps)),
+            dma((2, 2, steps, 2)),
+            dma((2, 2, steps, 2)),
             dma((2, NZ)),
             dma((2, NZ)),
             dma((2 * slots,)),
@@ -468,8 +475,8 @@
             dma((2 * slots,)),
             dma((2 * slots,)),
             dma((2, 2)),
-            dma((2, 2, steps)),
-            dma((2, 2, steps)),
+            dma((2, 2, steps, 2)),
+            dma((2, 2, steps, 2)),
             dma((7,)),
         ],
         compiler_params=pltpu.CompilerParams(

time: 111 us -> 110 us (level)
  the two profiles are of different devices: /device:TPU:44 before, /device:TPU:6 now
where the time goes in v5:
time: 110 us; the launch traced here: 109 us
  Pallas kernels  105 us (95%)
  other arithmetic  2.22 us (2%)
  between operations  1.43 us (1%)
    pallas_call x1, Pallas kernels, step(): pl.pallas_call(step_kernel, name='step', out_shape=(jax.ShapeDtypeStruct(...  105 us
    sub x1, other arithmetic, adam_update(): new_master = master - learn_rate * (ascent + decay_rate * master)  2.22 us

profile of v5, /device:TPU:6, one launch (start us, length us, event | category | flops | bytes accessed | tf_op | source)
XLA Modules:
  0.0 109.2 jit_solution(9009547462880100640)
XLA Ops:
  0.6 0.0 copy-start
  0.6 0.0 copy-start.2
  0.7 0.0 copy-start.3
  1.4 104.7 %step.1 = (bf16[384,768]{1,0:T(8,128)(2,1)}, f32[2,24,2048]{2,1,0:T(8,128)}) custom-call(s32[512]{0:T(512)} %place_ref.1, s32[4,128]{1,0:T(4,128)} %bitcast.1, s32[1]{0:T(128)S(6)} %copy.12.live_ref, bf16[384,768]{1,0:T(8,128)(2,1)} %acts_hbm.1, bf16[384,2048]{1,0:T(8,128)(2,1)} %out_hbm.1, f32[2,24,2048]{2,1,0:T(8,128)} %master_hbm.1), custom_call_target="tpu_custom_call" | custom-call | tf_op jit(solution)/shard_map/step/pallas_call | solution.py:436
  106.1 0.0 copy-start.1
  106.1 0.0 copy-done
  106.1 0.0 copy-done.2
  106.1 0.0 copy-done.3
  106.1 2.2 %multiply_subtract_fusion = (f32[2,24,2048]{2,1,0:T(8,128)}, f32[2,24,2048]{2,1,0:T(8,128)}, f32[2,24,2048]{2,1,0:T(8,128)}) fusion(f32[2,24,2048]{2,1,0:T(8,128)S(1)} %copy-done, f32[2,24,2048]{2,1,0:T(8,128)} %get-tuple-element.7, f32[2,24,2048]{2,1,0:T(8,128)S(1)} %copy-done.2, f32[2,24,2048]{2,1,0:T(8,128)S(1)} %copy-done.3), kind=kLoop, calls=%fused_computation.2 | loop fusion | flops 1376256 | bytes 2752512 | tf_op jit(solution)/shard_map/sub | solution.py:493
  108.3 0.0 copy-done.1
  108.3 0.8 copy.13
Async XLA Ops:
  0.6 105.5 %copy-start = (f32[2,24,2048]{2,1,0:T(8,128)S(1)}, f32[2,24,2048]{2,1,0:T(8,128)}, u32[]{:S(2)}) copy-start(f32[2,24,2048]{2,1,0:T(8,128)} %master_hbm.1) | copy-start | bytes 1179652
  0.6 105.5 %copy-start.2 = (f32[2,24,2048]{2,1,0:T(8,128)S(1)}, f32[2,24,2048]{2,1,0:T(8,128)}, u32[]{:S(2)}) copy-start(f32[2,24,2048]{2,1,0:T(8,128)} %param.13) | copy-start | bytes 1179652
  0.7 105.5 %copy-start.3 = (f32[2,24,2048]{2,1,0:T(8,128)S(1)}, f32[2,24,2048]{2,1,0:T(8,128)}, u32[]{:S(2)}) copy-start(f32[2,24,2048]{2,1,0:T(8,128)} %param.12) | copy-start | bytes 1179652
  106.1 2.3 %copy-start.1 = (bf16[384,768]{1,0:T(8,128)(2,1)S(1)}, bf16[384,768]{1,0:T(8,128)(2,1)}, u32[]{:S(2)}) copy-start(bf16[384,768]{1,0:T(8,128)(2,1)} %get-tuple-element.15) | copy-start | bytes 1769476

commit v6 on v5

--- a/solution.py
+++ b/solution.py
@@ -30,7 +30,7 @@
 
 
 def by_distance(places):
-    far = sorted(places, key=lambda d: (-min(d[0], NX - d[0]), abs(d[1]), d[1], d[0]))
+    far = sorted(places, key=lambda d: (min(d[0], NX - d[0]), abs(d[1]), d[1], d[0]))
     return [d for d in far if d != (0, 0)]
 
 
@@ -399,7 +399,7 @@
         rs_step(0, step)
 
     kept = lax.broadcasted_iota(jnp.int32, (acts_ref.shape[0], NY * rows), 0) < live_ref[0]
-    for i, dx in enumerate(sorted(range(NX), key=lambda d: (-min(d, NX - d), d))):
+    for i, dx in enumerate(sorted(range(NX), key=lambda d: (min(d, NX - d), d))):
         if i == NX - 1:
             rs_last(0)
             back.wait_recv()

time: 110 us -> 111 us (level)
  Pallas kernels: 105 us -> 107 us
    pallas_call x1, Pallas kernels: 105 us -> 107 us  [step(): pl.pallas_call(step_kernel, name='step', out_shape=(jax.ShapeDtypeStruct(...]
where the time goes in v6:
time: 111 us
  Pallas kernels  107 us (96%)
  other arithmetic  2.22 us (2%)
  between operations  1.43 us (1%)
    pallas_call x1, Pallas kernels, step(): pl.pallas_call(step_kernel, name='step', out_shape=(jax.ShapeDtypeStruct(...  107 us
    sub x1, other arithmetic, adam_update(): new_master = master - learn_rate * (ascent + decay_rate * master)  2.22 us

profile of v6, /device:TPU:6, one launch (start us, length us, event | category | flops | bytes accessed | tf_op | source)
XLA Modules:
  0.0 111.2 jit_solution(8227671668657005483)
XLA Ops:
  0.6 0.0 copy-start
  0.6 0.0 copy-start.2
  0.7 0.0 copy-start.3
  1.4 106.7 %step.1 = (bf16[384,768]{1,0:T(8,128)(2,1)}, f32[2,24,2048]{2,1,0:T(8,128)}) custom-call(s32[512]{0:T(512)} %place_ref.1, s32[4,128]{1,0:T(4,128)} %bitcast.1, s32[1]{0:T(128)S(6)} %copy.12.live_ref, bf16[384,768]{1,0:T(8,128)(2,1)} %acts_hbm.1, bf16[384,2048]{1,0:T(8,128)(2,1)} %out_hbm.1, f32[2,24,2048]{2,1,0:T(8,128)} %master_hbm.1), custom_call_target="tpu_custom_call" | custom-call | tf_op jit(solution)/shard_map/step/pallas_call | solution.py:436
  108.1 0.0 copy-start.1
  108.2 0.0 copy-done
  108.2 0.0 copy-done.2
  108.2 0.0 copy-done.3
  108.2 2.2 %multiply_subtract_fusion = (f32[2,24,2048]{2,1,0:T(8,128)}, f32[2,24,2048]{2,1,0:T(8,128)}, f32[2,24,2048]{2,1,0:T(8,128)}) fusion(f32[2,24,2048]{2,1,0:T(8,128)S(1)} %copy-done, f32[2,24,2048]{2,1,0:T(8,128)} %get-tuple-element.7, f32[2,24,2048]{2,1,0:T(8,128)S(1)} %copy-done.2, f32[2,24,2048]{2,1,0:T(8,128)S(1)} %copy-done.3), kind=kLoop, calls=%fused_computation.2 | loop fusion | flops 1376256 | bytes 2752512 | tf_op jit(solution)/shard_map/sub | solution.py:493
  110.4 0.0 copy-done.1
  110.4 0.8 copy.13
Async XLA Ops:
  0.6 107.5 %copy-start = (f32[2,24,2048]{2,1,0:T(8,128)S(1)}, f32[2,24,2048]{2,1,0:T(8,128)}, u32[]{:S(2)}) copy-start(f32[2,24,2048]{2,1,0:T(8,128)} %master_hbm.1) | copy-start | bytes 1179652
  0.6 107.5 %copy-start.2 = (f32[2,24,2048]{2,1,0:T(8,128)S(1)}, f32[2,24,2048]{2,1,0:T(8,128)}, u32[]{:S(2)}) copy-start(f32[2,24,2048]{2,1,0:T(8,128)} %param.13) | copy-start | bytes 1179652
  0.7 107.5 %copy-start.3 = (f32[2,24,2048]{2,1,0:T(8,128)S(1)}, f32[2,24,2048]{2,1,0:T(8,128)}, u32[]{:S(2)}) copy-start(f32[2,24,2048]{2,1,0:T(8,128)} %param.12) | copy-start | bytes 1179652
  108.1 2.3 %copy-start.1 = (bf16[384,768]{1,0:T(8,128)(2,1)S(1)}, bf16[384,768]{1,0:T(8,128)(2,1)}, u32[]{:S(2)}) copy-start(bf16[384,768]{1,0:T(8,128)(2,1)} %get-tuple-element.15) | copy-start | bytes 1769476
